TPU v7x, 128 devices: a whole 4x4x4 slice. The times are simulated.
128 devices in a mesh: child: 2 (over core), rows: 64 (over z, y, x).
Axes of the slice: x: 4, y: 4, z: 4, core: 2. Of those that a mesh axis runs over, the one named last changes fastest.
Arguments:
- front_update: bfloat16 [2, 12288, 61440], P('child', 'rows'), may hold values from -0.0234375 to 0.0234375
- child_omega: bfloat16 [2, 61440, 256], P('child', 'rows'), may hold values from -6 to 6
- parent_block: bfloat16 [49152, 128], P(('child', 'rows')), may hold values from -0.5 to 0.5
- parent_omega: bfloat16 [49152, 256], P(('child', 'rows')), may hold values from -6 to 6
- child_map: int32 [2, 12288], replicated, may hold values from 0 to 49151, as said below
- leaf_order: int32 [49152], replicated, may hold values from 0 to 49151, as said below
Outputs:
- parent_samples: float32 [49152, 256], P(('child', 'rows'))
Inputs may be any that keep to these rules, and one draw needn't show every extreme that they name: `child_map`: within one child the entries are distinct. Of each aligned block of 192 rows of one child, at most 3 entries fall in any one aligned block of 384 parent rows, and some block of parent rows gets exactly 3 from every such block. `leaf_order`: A permutation. Each aligned block of 384 leaf positions holds exactly 3 rows of every aligned block of 384 natural rows.
All inputs are finite; a program needn't handle non-finite values.
Results may differ from a plain program's by a relative error of at most 0.0003.
Values may be sent and summed in bfloat16 or wider, within the bound.
A program may use at most 192 MiB of HBM per device.

v0:
```python
import jax
import jax.numpy as jnp
from jax import lax
from jax.sharding import PartitionSpec as P


def split_up(value, dim, length):
    before, after = (value.shape[:dim], value.shape[dim + 1 :])
    return jnp.moveaxis(value.reshape(*before, length, -1, *after), dim, 0)


def in_order(blocks, dim):
    blocks = jnp.moveaxis(blocks, 0, dim)
    lengths = blocks.shape
    return blocks.reshape(*lengths[:dim], lengths[dim] * lengths[dim + 1], *lengths[dim + 2 :])


def one_exchange(value, axis, axes, splits, concats):
    sizes = [lax.axis_size(a) for a in axes]
    blocks = split_up(value, splits[0], sizes[0])
    blocks = jnp.moveaxis(split_up(blocks, splits[1] + 1, sizes[1]), 0, 1)
    inside = blocks.shape[2:]
    blocks = blocks.reshape(-1, *inside)
    blocks = lax.all_to_all(blocks, axis, split_axis=0, concat_axis=0, tiled=True)
    blocks = in_order(blocks.reshape(*sizes, *inside), concats[0] + 1)
    return in_order(blocks, concats[1])


def bucket_rank(owner_ids, owners):
    one_hot = (owner_ids[:, None] == jnp.arange(owners, dtype=jnp.int32)[None, :]).astype(jnp.int32)
    running = jnp.cumsum(one_hot, axis=0)
    return jnp.sum(one_hot * running, axis=1) - 1


def select_rows(targets, total, values):
    picker = (targets[None, :] == jnp.arange(total, dtype=jnp.int32)[:, None]).astype(jnp.float32)
    return jnp.dot(
        picker, values, precision=lax.Precision.HIGHEST, preferred_element_type=jnp.float32
    )


def pick_rows(sources, values):
    picker = (sources[:, None] == jnp.arange(values.shape[0], dtype=jnp.int32)[None, :]).astype(
        jnp.float32
    )
    return jnp.dot(
        picker, values, precision=lax.Precision.HIGHEST, preferred_element_type=jnp.float32
    )


def body(front_update, child_omega, parent_block, parent_omega, child_map, leaf_order):
    children = lax.axis_size("child")
    row_count = lax.axis_size("rows")
    owners = children * row_count
    device_id = lax.axis_index("child") * row_count + lax.axis_index("rows")
    slab_rows = front_update[0]
    local_rows = slab_rows.shape[0]
    sample_cols = child_omega.shape[2]
    sampled = jnp.dot(
        slab_rows,
        lax.all_gather(child_omega, "rows", axis=1, tiled=True)[0],
        preferred_element_type=jnp.float32,
    )
    parent_dev = parent_block.shape[0]
    capacity = 2 * local_rows // owners
    route_table = child_map.reshape(owners, local_rows)
    my_targets = lax.dynamic_index_in_dim(route_table, device_id, 0, keepdims=False)
    target_owner = my_targets // parent_dev
    target_slot = target_owner * capacity + bucket_rank(target_owner, owners)
    outgoing = select_rows(target_slot, owners * capacity, sampled)
    incoming = one_exchange(
        outgoing.reshape(children, row_count, capacity, sample_cols),
        ("child", "rows"),
        ("child", "rows"),
        (0, 1),
        (0, 1),
    )
    incoming = incoming.reshape(owners * capacity, sample_cols)
    arrives = route_table // parent_dev == device_id
    arrive_rank = jnp.cumsum(arrives.astype(jnp.int32), axis=1) - 1
    slot_column = jnp.where(arrives, arrive_rank, capacity)
    local_target = jnp.where(arrives, route_table % parent_dev, parent_dev)
    source_ids = jnp.broadcast_to(jnp.arange(owners, dtype=jnp.int32)[:, None], route_table.shape)
    places = (
        jnp.full((owners, capacity + 1), parent_dev, jnp.int32)
        .at[source_ids, slot_column]
        .set(local_target)[:, :capacity]
    )
    assembled = select_rows(places.reshape(-1), parent_dev, incoming)
    leaf_size = parent_block.shape[1]
    leaf_blocks = parent_dev // leaf_size
    own_samples = jnp.einsum(
        "bij,bjr->bir",
        parent_block.reshape(leaf_blocks, leaf_size, leaf_size),
        parent_omega.reshape(leaf_blocks, leaf_size, sample_cols),
        preferred_element_type=jnp.float32,
    ).reshape(parent_dev, sample_cols)
    assembled = assembled + own_samples
    parent_rows = leaf_order.shape[0]
    position = (
        jnp.zeros((parent_rows,), jnp.int32)
        .at[leaf_order]
        .set(jnp.arange(parent_rows, dtype=jnp.int32))
    )
    my_positions = lax.dynamic_slice_in_dim(position, device_id * parent_dev, parent_dev)
    leaf_owner = my_positions // parent_dev
    leaf_capacity = parent_dev // owners
    leaf_slot = leaf_owner * leaf_capacity + bucket_rank(leaf_owner, owners)
    sending = select_rows(leaf_slot, owners * leaf_capacity, assembled)
    arrived = lax.all_to_all(
        sending.reshape(owners, leaf_capacity, sample_cols),
        ("child", "rows"),
        split_axis=0,
        concat_axis=0,
        tiled=True,
    )
    arrived = arrived.reshape(owners * leaf_capacity, sample_cols)
    natural = lax.dynamic_slice_in_dim(leaf_order, device_id * parent_dev, parent_dev)
    anchor = natural // parent_dev
    offset = natural % parent_dev
    same_anchor = anchor[:, None] == anchor[None, :]
    earlier = offset[None, :] < offset[:, None]
    arrival_rank = jnp.sum((same_anchor & earlier).astype(jnp.int32), axis=1)
    return pick_rows(anchor * leaf_capacity + arrival_rank, arrived)


def solution(mesh):
    placed = (
        P("child", "rows", None),
        P("child", "rows", None),
        P(("child", "rows"), None),
        P(("child", "rows"), None),
        P(),
        P(),
    )
    return jax.shard_map(
        body, mesh=mesh, in_specs=placed, out_specs=P(("child", "rows"), None), check_vma=False
    )
```

profile of v0, /device:TPU:1, one launch (start us, length us, event | category | flops | bytes accessed | tf_op | source)
XLA Modules:
  0.0 357.9 jit_solution(657947989625577888)
XLA Ops:
  6.5 0.0 copy-start
  6.5 0.0 all-gather.2.cloned.1.call-start
  6.5 0.7 all-gather.2.cloned.1.call-update
  7.3 1.0 reshape.119
  8.4 0.1 iota_compare_fusion.11
  8.5 0.1 fusion.16
  8.7 0.2 fusion.14
  8.9 0.1 reshape.147
  9.0 0.1 copy.37
  9.1 0.1 fusion.18
  9.3 0.1 copy.46
  9.5 0.8 multiply_reduce_fusion
  10.3 0.8 and_reduce_fusion
  11.1 0.1 reshape.145
  11.2 90.2 %scatter_custom_fusion.1 = s32[512]{0:T(512)S(1)} fusion(s32[24576]{0:T(1024)S(1)} %reshape.145, s32[24576]{0:T(1024)S(1)} %reshape.147, s32[]{:T(128)} %constant.80.clone.1), kind=kCustom, calls=%fused_computation.74 | custom fusion | bytes 2052
  101.3 0.1 copy.41
  101.5 0.2 eq.140
  101.7 1.0 compare_select_fusion
  102.6 179.9 %scatter_custom_fusion = s32[49152]{0:T(1024)S(1)} fusion(s32[49152]{0:T(1024)S(1)} %compare_select_fusion, s32[49152]{0:T(1024)S(1)} %iota.32, s32[]{:T(128)} %constant.81.clone.1), kind=kCustom, calls=%fused_computation.50 | custom fusion | bytes 196612 | tf_op jit(solution)/shard_map/scatter | solution.py:103
  282.6 0.8 add_select_fusion.4
  283.4 0.1 copy.35
  283.5 0.2 fusion.9
  283.7 0.1 broadcast_add_fusion
  283.8 0.2 fusion.22
  284.0 0.2 fusion.11
  284.3 0.0 copy-start.1
  284.3 0.0 all-gather.2.cloned.1.call-done
  284.3 19.9 %fusion = f32[192,256]{1,0:T(8,128)S(1)} fusion(bf16[1,61440,256]{2,1,0:T(8,128)(2,1)} %all-gather.2.cloned.1.call-done, bf16[1,192,61440]{2,1,0:T(8,128)(2,1)} %param.6), kind=kOutput, calls=%fused_computation.2 | convolution fusion | flops 6039797760 | bytes 55246848 | tf_op jit(solution)/shard_map/dot_general | solution.py:59
  304.2 0.3 fusion.5
  304.6 1.1 reshape_transpose_transpose_reshape_reshape_reshape.4
  305.7 11.5 %all-to-all-start = ((f32[128,1,1,3,256]{4,2,3,1,0:T(1,128)}), f32[128,1,1,3,256]{4,2,3,1,0:T(1,128)S(1)}, u32[]{:S(2)}, u32[]{:S(2)}) async-start(f32[128,1,1,3,256]{4,2,3,1,0:T(1,128)} %reshape_transpose_transpose_reshape_reshape_reshape.4), calls=%async_computation | async-start | bytes 786432 | tf_op jit(solution)/shard_map/all_to_all | solution.py:24
  317.3 0.0 copy-done
  317.3 0.0 copy-done.1
  317.3 0.2 fusion.33
  317.5 12.0 %all-to-all-done = f32[128,1,1,3,256]{4,2,3,1,0:T(1,128)S(1)} async-done(((f32[128,1,1,3,256]{4,2,3,1,0:T(1,128)}), f32[128,1,1,3,256]{4,2,3,1,0:T(1,128)S(1)}, u32[]{:S(2)}, u32[]{:S(2)}) %all-to-all-start) | async-done | bytes 393248 | tf_op jit(solution)/shard_map/all_to_all | solution.py:24
  329.4 0.1 copy.52
  329.6 0.2 reshape_reshape.3
  329.8 0.5 convolution_add_fusion
  330.3 0.5 fusion.4
  330.8 1.0 reshape.129
  331.8 4.2 %all-to-all-start.1 = ((f32[128,3,256]{2,1,0:T(4,128)}), f32[128,3,256]{2,1,0:T(4,128)S(1)}, u32[]{:S(2)}, u32[]{:S(2)}) async-start(f32[128,3,256]{2,1,0:T(4,128)} %reshape.129), calls=%async_computation.1 | async-start | bytes 1048576 | tf_op jit(solution)/shard_map/all_to_all | solution.py:110
  335.9 0.3 convert_reduce_fusion
  336.2 13.4 %all-to-all-done.1 = f32[128,3,256]{2,1,0:T(4,128)S(1)} async-done(((f32[128,3,256]{2,1,0:T(4,128)}), f32[128,3,256]{2,1,0:T(4,128)S(1)}, u32[]{:S(2)}, u32[]{:S(2)}) %all-to-all-start.1) | async-done | bytes 393248 | tf_op jit(solution)/shard_map/all_to_all | solution.py:110
  349.6 0.2 reshape.130
  349.8 1.3 fusion.3
  (29 shorter events, 0.4 us)
Async XLA Ops:
  6.5 310.7 %copy-start = (bf16[384,256]{1,0:T(8,128)(2,1)S(1)}, bf16[384,256]{1,0:T(8,128)(2,1)}, u32[]{:S(2)}) copy-start(bf16[384,256]{1,0:T(8,128)(2,1)} %param.9) | copy-start | bytes 589828
  6.5 277.8 %all-gather.2.cloned.1.call-start = ((), (), s32[]{:S(2)}) async-start(), calls=%async_computation.2 | async-start | bytes 31948800 | tf_op jit(solution)/shard_map/all_gather | solution.py:61
  284.3 33.0 %copy-start.1 = (bf16[384,128]{1,0:T(8,128)(2,1)S(1)}, bf16[384,128]{1,0:T(8,128)(2,1)}, u32[]{:S(2)}) copy-start(bf16[384,128]{1,0:T(8,128)(2,1)} %param.8) | copy-start | bytes 294916
  305.7 23.7 %all-to-all-start = ((f32[128,1,1,3,256]{4,2,3,1,0:T(1,128)}), f32[128,1,1,3,256]{4,2,3,1,0:T(1,128)S(1)}, u32[]{:S(2)}, u32[]{:S(2)}) async-start(f32[128,1,1,3,256]{4,2,3,1,0:T(1,128)} %reshape_transpose_transpose_reshape_reshape_reshape.4), calls=%async_computation | async-start | bytes 786432 | tf_op jit(solution)/shard_map/all_to_all | solution.py:24
  331.8 17.8 %all-to-all-start.1 = ((f32[128,3,256]{2,1,0:T(4,128)}), f32[128,3,256]{2,1,0:T(4,128)S(1)}, u32[]{:S(2)}, u32[]{:S(2)}) async-start(f32[128,3,256]{2,1,0:T(4,128)} %reshape.129), calls=%async_computation.1 | async-start | bytes 1048576 | tf_op jit(solution)/shard_map/all_to_all | solution.py:110
Sparse Core Ops, SparseCore 0:
  10.1 156.1 all-gather.1
where the time goes:
time: 358 us
  local copies, waits for them, and re-layouts  275 us (77%)
  waiting for transfers between devices  26 us (7%)
  matrix products  22.8 us (6%)
  starting transfers between devices  15.7 us (4%)
  between operations  13.7 us (4%)
  other arithmetic  5.04 us (1%)
    scatter x1, local copies, waits for them, and re-layouts, body(): position = jnp.zeros((parent_rows,), jnp.int32).at[leaf_order].set(jnp.ar...  180 us
    unnamed x9, local copies, waits for them, and re-layouts  90.4 us
    dot_general x1, matrix products, body(): jnp.dot(slab_rows, lax.all_gather(child_omega, 'rows', axis=1, tiled=True...  19.9 us
    all_to_all x1, waiting for transfers between devices, body(): lax.all_to_all(sending.reshape(owners, leaf_capacity, sample_cols), ('chi...  13.4 us
    all_to_all x1, waiting for transfers between devices, one_exchange(): lax.all_to_all(blocks, axis, split_axis=0, concat_axis=0, tiled=True)  12 us
    all_to_all x1, starting transfers between devices, one_exchange(): lax.all_to_all(blocks, axis, split_axis=0, concat_axis=0, tiled=True)  11.5 us
  transfers between devices with their start and end apart: 3, of which 2 were waited for; matrix products, arithmetic and copies ran while one was open for 77% of the time, Pallas kernels for 0%

commit v1 on v0

--- a/solution.py
+++ b/solution.py
@@ -48,6 +48,17 @@
     )
 
 
+def ranked(marked, values, capacity, empty):
+    length = marked.shape[1]
+    upto = jnp.tril(jnp.ones((length, length), jnp.bfloat16)).T
+    rank = jnp.dot(marked.astype(jnp.bfloat16), upto, preferred_element_type=jnp.float32)
+    rank = jnp.where(marked, rank.astype(jnp.int32), 0)
+    kept = [
+        jnp.sum(jnp.where(rank == k + 1, values - empty, 0), axis=1) + empty for k in range(capacity)
+    ]
+    return jnp.stack(kept, axis=1)
+
+
 def body(front_update, child_omega, parent_block, parent_omega, child_map, leaf_order):
     children = lax.axis_size("child")
     row_count = lax.axis_size("rows")
@@ -77,15 +88,7 @@
     )
     incoming = incoming.reshape(owners * capacity, sample_cols)
     arrives = route_table // parent_dev == device_id
-    arrive_rank = jnp.cumsum(arrives.astype(jnp.int32), axis=1) - 1
-    slot_column = jnp.where(arrives, arrive_rank, capacity)
-    local_target = jnp.where(arrives, route_table % parent_dev, parent_dev)
-    source_ids = jnp.broadcast_to(jnp.arange(owners, dtype=jnp.int32)[:, None], route_table.shape)
-    places = (
-        jnp.full((owners, capacity + 1), parent_dev, jnp.int32)
-        .at[source_ids, slot_column]
-        .set(local_target)[:, :capacity]
-    )
+    places = ranked(arrives, route_table % parent_dev, capacity, parent_dev)
     assembled = select_rows(places.reshape(-1), parent_dev, incoming)
     leaf_size = parent_block.shape[1]
     leaf_blocks = parent_dev // leaf_size
@@ -96,17 +99,10 @@
         preferred_element_type=jnp.float32,
     ).reshape(parent_dev, sample_cols)
     assembled = assembled + own_samples
-    parent_rows = leaf_order.shape[0]
-    position = (
-        jnp.zeros((parent_rows,), jnp.int32)
-        .at[leaf_order]
-        .set(jnp.arange(parent_rows, dtype=jnp.int32))
-    )
-    my_positions = lax.dynamic_slice_in_dim(position, device_id * parent_dev, parent_dev)
-    leaf_owner = my_positions // parent_dev
     leaf_capacity = parent_dev // owners
-    leaf_slot = leaf_owner * leaf_capacity + bucket_rank(leaf_owner, owners)
-    sending = select_rows(leaf_slot, owners * leaf_capacity, assembled)
+    leaf_table = leaf_order.reshape(owners, parent_dev)
+    leaving = ranked(leaf_table // parent_dev == device_id, leaf_table % parent_dev, leaf_capacity, 0)
+    sending = pick_rows(leaving.reshape(-1), assembled)
     arrived = lax.all_to_all(
         sending.reshape(owners, leaf_capacity, sample_cols),
         ("child", "rows"),
@@ -117,9 +113,9 @@
     arrived = arrived.reshape(owners * leaf_capacity, sample_cols)
     natural = lax.dynamic_slice_in_dim(leaf_order, device_id * parent_dev, parent_dev)
     anchor = natural // parent_dev
-    offset = natural % parent_dev
     same_anchor = anchor[:, None] == anchor[None, :]
-    earlier = offset[None, :] < offset[:, None]
+    place = jnp.arange(parent_dev, dtype=jnp.int32)
+    earlier = place[None, :] < place[:, None]
     arrival_rank = jnp.sum((same_anchor & earlier).astype(jnp.int32), axis=1)
     return pick_rows(anchor * leaf_capacity + arrival_rank, arrived)
 

time: 358 us -> 237 us (0.66)
  local copies, waits for them, and re-layouts: 275 us -> 4.57 us
  waiting for transfers between devices: 26 us -> 178 us
    scatter x1 -> x0, local copies, waits for them, and re-layouts: 180 us -> none  [body(): position = jnp.zeros((parent_rows,), jnp.int32).at[leaf_order].set(jnp.ar...]
    all_gather x1, waiting for transfers between devices: 0.02 us -> 154 us  [body(): lax.all_gather(child_omega, 'rows', axis=1, tiled=True)[0]]
    unnamed x9 -> x5, local copies, waits for them, and re-layouts: 90.4 us -> 0.02 us
  transfers between devices with their start and end apart: 3 -> 3, of which waited for: 2 -> 3; matrix products, arithmetic and copies ran while one was open for 77% -> 3% of each run, Pallas kernels for 0% -> 0%
where the time goes in v1:
time: 237 us; the launch traced here: 236 us
  waiting for transfers between devices  178 us (75%)
  matrix products  23.5 us (10%)
  between operations  13.6 us (6%)
  starting transfers between devices  12.2 us (5%)
  local copies, waits for them, and re-layouts  4.57 us (2%)
  other arithmetic  4.4 us (2%)
    all_gather x1, waiting for transfers between devices, body(): lax.all_gather(child_omega, 'rows', axis=1, tiled=True)[0]  154 us
    dot_general x1, matrix products, body(): jnp.dot(slab_rows, lax.all_gather(child_omega, 'rows', axis=1, tiled=True...  19.9 us
    all_to_all x1, waiting for transfers between devices, body(): lax.all_to_all(sending.reshape(owners, leaf_capacity, sample_cols), ('chi...  11.8 us
    all_to_all x1, waiting for transfers between devices, one_exchange(): lax.all_to_all(blocks, axis, split_axis=0, concat_axis=0, tiled=True)  11.3 us
    all_to_all x1, starting transfers between devices, one_exchange(): lax.all_to_all(blocks, axis, split_axis=0, concat_axis=0, tiled=True)  8.02 us
  transfers between devices with their start and end apart: 3, of which 3 were waited for; matrix products, arithmetic and copies ran while one was open for 3% of the time, Pallas kernels for 0%

profile of v1, /device:TPU:1, one launch (start us, length us, event | category | flops | bytes accessed | tf_op | source)
XLA Modules:
  0.0 236.4 jit_solution(4879814055404891901)
XLA Ops:
  6.5 0.0 copy-start
  6.5 0.0 all-gather.2.cloned.1.call-start
  6.5 0.7 all-gather.2.cloned.1.call-update
  7.3 1.0 sign_compare_fusion
  8.3 0.1 ne.99
  8.3 1.0 reshape.112
  9.3 0.1 copy.24
  9.5 0.1 iota_compare_fusion.11
  9.6 0.1 fusion.21
  9.9 1.0 broadcast_remainder_fusion
  11.0 0.2 fusion.26
  11.2 0.3 select_reduce_fusion.5
  11.5 0.4 select_reduce_fusion.2
  11.9 0.0 copy-start.1
  12.0 154.3 %all-gather.2.cloned.1.call-done = bf16[1,61440,256]{2,1,0:T(8,128)(2,1)} async-done(((bf16[1,960,256]{2,1,0:T(8,128)(2,1)}), bf16[1,61440,256]{2,1,0:T(8,128)(2,1)}) %all-gather.2.cloned.1.call-update) | async-done | bytes 31457296 | tf_op jit(solution)/shard_map/all_gather | solution.py:72
  166.3 19.9 %fusion = f32[192,256]{1,0:T(8,128)S(1)} fusion(bf16[1,61440,256]{2,1,0:T(8,128)(2,1)} %all-gather.2.cloned.1.call-done, bf16[1,192,61440]{2,1,0:T(8,128)(2,1)} %param.6), kind=kOutput, calls=%fused_computation | convolution fusion | flops 6039797760 | bytes 55246848 | tf_op jit(solution)/shard_map/dot_general | solution.py:70
  186.2 0.3 fusion.9
  186.5 1.1 reshape_transpose_transpose_reshape_reshape_reshape.4
  187.7 8.0 %all-to-all-start = ((f32[128,1,1,3,256]{4,2,3,1,0:T(1,128)}), f32[128,1,1,3,256]{4,2,3,1,0:T(1,128)S(1)}, u32[]{:S(2)}, u32[]{:S(2)}) async-start(f32[128,1,1,3,256]{4,2,3,1,0:T(1,128)} %reshape_transpose_transpose_reshape_reshape_reshape.4), calls=%async_computation | async-start | bytes 786432 | tf_op jit(solution)/shard_map/all_to_all | solution.py:24
  195.7 0.1 copy.27
  195.8 0.2 eq.155
  196.0 0.1 copy.23
  196.1 0.2 eq.145
  196.4 0.0 copy-done
  196.4 0.0 copy-done.1
  196.4 0.2 fusion.52
  196.6 11.3 %all-to-all-done = f32[128,1,1,3,256]{4,2,3,1,0:T(1,128)S(1)} async-done(((f32[128,1,1,3,256]{4,2,3,1,0:T(1,128)}), f32[128,1,1,3,256]{4,2,3,1,0:T(1,128)S(1)}, u32[]{:S(2)}, u32[]{:S(2)}) %all-to-all-start) | async-done | bytes 393248 | tf_op jit(solution)/shard_map/all_to_all | solution.py:24
  207.9 0.1 copy.35
  208.0 0.2 reshape_reshape.3
  208.2 0.5 convolution_add_fusion
  208.7 0.5 fusion.8
  209.3 1.0 reshape.120
  210.2 4.2 %all-to-all-start.1 = ((f32[128,3,256]{2,1,0:T(4,128)}), f32[128,3,256]{2,1,0:T(4,128)S(1)}, u32[]{:S(2)}, u32[]{:S(2)}) async-start(f32[128,3,256]{2,1,0:T(4,128)} %reshape.120), calls=%async_computation.1 | async-start | bytes 1048576 | tf_op jit(solution)/shard_map/all_to_all | solution.py:106
  214.4 0.8 add_select_fusion.4
  215.2 0.2 convert_reduce_fusion
  215.4 0.8 multiply_add_fusion
  216.2 11.8 %all-to-all-done.1 = f32[128,3,256]{2,1,0:T(4,128)S(1)} async-done(((f32[128,3,256]{2,1,0:T(4,128)}), f32[128,3,256]{2,1,0:T(4,128)S(1)}, u32[]{:S(2)}, u32[]{:S(2)}) %all-to-all-start.1) | async-done | bytes 393248 | tf_op jit(solution)/shard_map/all_to_all | solution.py:106
  228.0 0.2 reshape.121
  228.2 1.3 fusion.6
  (18 shorter events, 0.3 us)
Async XLA Ops:
  6.5 189.8 %copy-start = (bf16[384,256]{1,0:T(8,128)(2,1)S(1)}, bf16[384,256]{1,0:T(8,128)(2,1)}, u32[]{:S(2)}) copy-start(bf16[384,256]{1,0:T(8,128)(2,1)} %param.9) | copy-start | bytes 589828
  6.5 159.7 %all-gather.2.cloned.1.call-start = ((), (), s32[]{:S(2)}) async-start(), calls=%async_computation.2 | async-start | bytes 31948800 | tf_op jit(solution)/shard_map/all_gather | solution.py:72
  11.9 184.4 %copy-start.1 = (bf16[384,128]{1,0:T(8,128)(2,1)S(1)}, bf16[384,128]{1,0:T(8,128)(2,1)}, u32[]{:S(2)}) copy-start(bf16[384,128]{1,0:T(8,128)(2,1)} %param.8) | copy-start | bytes 294916
  187.7 20.2 %all-to-all-start = ((f32[128,1,1,3,256]{4,2,3,1,0:T(1,128)}), f32[128,1,1,3,256]{4,2,3,1,0:T(1,128)S(1)}, u32[]{:S(2)}, u32[]{:S(2)}) async-start(f32[128,1,1,3,256]{4,2,3,1,0:T(1,128)} %reshape_transpose_transpose_reshape_reshape_reshape.4), calls=%async_computation | async-start | bytes 786432 | tf_op jit(solution)/shard_map/all_to_all | solution.py:24
  210.2 17.8 %all-to-all-start.1 = ((f32[128,3,256]{2,1,0:T(4,128)}), f32[128,3,256]{2,1,0:T(4,128)S(1)}, u32[]{:S(2)}, u32[]{:S(2)}) async-start(f32[128,3,256]{2,1,0:T(4,128)} %reshape.120), calls=%async_computation.1 | async-start | bytes 1048576 | tf_op jit(solution)/shard_map/all_to_all | solution.py:106
Sparse Core Ops, SparseCore 0:
  10.1 156.1 all-gather.1

commit v2 on v1

v2 whole, which is shorter than its diff:
```python
import functools

import jax
import jax.numpy as jnp
from jax import lax
from jax.experimental import pallas as pl
from jax.experimental.pallas import tpu as pltpu
from jax.sharding import PartitionSpec as P

MESH = pl.DeviceIdType.MESH
SIDE = 4
CHIPS = SIDE**3
OWNERS = 2 * CHIPS
SHARD = 960
PIECE = 160
PAIR = 2 * SHARD
CAP = 3
TILE = 8
WINDOW = 4
ORDERS = ((0, 1, 2), (1, 2, 0), (2, 0, 1))
BATCHES = (
    (0, 3, 3, 0, 0),
    (1, 3, 1, 0, 0),
    (1, 3, 1, 0, 1),
    (1, 3, 1, 0, 2),
    (0, 3, 1, 0, 3),
    (0, 1, 3, 3, 0),
    (1, 3, 1, 0, 3),
    (1, 1, 3, 3, 0),
    (0, 1, 1, 3, 3),
    (1, 1, 1, 3, 3),
)
WALK = (0, 1, 3, 2)


def moved(offset, dim, by):
    new = list(offset)
    new[dim] = (new[dim] + by) % SIDE
    return tuple(new)


def all_sends():
    sends = {(d, sign): [] for d in range(3) for sign in (1, -1)}
    for part, order in enumerate(ORDERS):
        for half, turn in enumerate((1, -1)):
            for phase in range(3):
                here = order[phase]
                for a in WALK:
                    for b in WALK:
                        inner = (a, b)
                        if any(inner[i] for i in range(2) if i >= phase):
                            continue
                        offset = [0, 0, 0]
                        for i in range(phase):
                            offset[order[i]] = inner[i]
                        for sign in (1, -1):
                            sends[here, sign].append((phase, 0, WALK.index(b), WALK.index(a), half, tuple(offset), part))
                        offset[here] = turn % SIDE
                        sends[here, turn].append((phase, 1, WALK.index(b), WALK.index(a), half, tuple(offset), part))
    return {link: sorted(found) for link, found in sends.items()}


def make_schedule(window):
    waiting = all_sends()
    links = list(waiting)
    arrived = {((0, 0, 0), part, half): -window for part in range(3) for half in range(2)}
    slots = []
    while any(waiting.values()):
        now, came = [], []
        for link in links:
            ready = [s for s in waiting[link] if arrived.get((s[5], s[6], s[4]), 10**6) + window <= len(slots)]
            assert ready
            chosen = ready[0]
            waiting[link].remove(chosen)
            now.append((link, chosen[5], chosen[6], chosen[4]))
            came.append((moved(chosen[5], *link), chosen[6], chosen[4]))
        for key in came:
            assert key not in arrived
            arrived[key] = len(slots)
        slots.append(now)
    return slots, arrived


def batch_members(batch):
    other, ny, nz, y0, z0 = batch
    return [(other, WALK[y0 + i % ny], WALK[z0 + i // ny]) for i in range(ny * nz)]


def ready_slot(batch, arrived):
    latest = 0
    for other, ry, rz in batch_members(batch):
        for rx in ((2, 1, 3) if other else (0, 1, 3)):
            for part in range(3):
                for half in range(2):
                    latest = max(latest, arrived[(rx, ry, rz), part, half])
    return latest


def two_parts(values):
    high = values.astype(jnp.bfloat16)
    low = (values - high.astype(jnp.float32)).astype(jnp.bfloat16)
    return jnp.concatenate([high, low], axis=-1)


def picked(picker, parts):
    both = jnp.dot(picker, parts, preferred_element_type=jnp.float32)
    return both[:, :128] + both[:, 128:]


def kernel(
    front, omega, block, parent_omega, t1, t2, t3, t4, out,
    gathered, slab, total, stacked, parts, send1, recv1, send2, recv2, p1, p2, p3, p4,
    own_sem, slab_sem, sent_sem, slot_sem, mate_sem, sent1, came1, sent2, came2,
):
    child = lax.axis_index("child")
    chip = lax.axis_index("rows")
    me = child * CHIPS + chip
    place = (lax.rem(chip, SIDE), lax.rem(chip // SIDE, SIDE), chip // (SIDE * SIDE))
    back = [[lax.rem(place[d] + SIDE - r, SIDE) for r in range(SIDE)] for d in range(3)]

    def chip_at(xyz):
        return xyz[2] * (SIDE * SIDE) + xyz[1] * SIDE + xyz[0]

    def source(offset):
        return chip_at([back[d][offset[d]] for d in range(3)])

    neighbour = {}
    for d in range(3):
        for sign in (1, -1):
            offset = [0, 0, 0]
            offset[d] = -sign % SIDE
            neighbour[d, sign] = source(offset)

    own = pltpu.make_async_copy(omega.at[0], gathered.at[pl.ds(chip * SHARD, SHARD)], own_sem)
    own.start()
    barrier = pltpu.get_barrier_semaphore()
    for there in neighbour.values():
        pl.semaphore_signal(barrier, inc=1, device_id=(child, there), device_id_type=MESH)
    pl.semaphore_signal(barrier, inc=1, device_id=(1 - child, chip), device_id_type=MESH)

    def walk(i):
        return i + i // 2 - 2 * (i // 3)

    def pair_of(batch, i):
        other, ny, nz, y0, z0 = batch
        y = lax.rem(place[1] + SIDE - walk(y0 + lax.rem(i, ny)), SIDE)
        z = lax.rem(place[2] + SIDE - walk(z0 + i // ny), SIDE)
        half = place[0] // 2
        half = 1 - half if other else half
        return (z * SIDE + y) * 2 + half

    def slab_copy(batch, first, i):
        columns = pl.ds(pl.multiple_of(pair_of(batch, i) * PAIR, PAIR), PAIR)
        return pltpu.make_async_copy(front.at[0, :, columns], slab.at[first + i], slab_sem.at[first + i])

    firsts, count = [], 0
    for batch in BATCHES:
        firsts.append(count)

        def start(i, carry, batch=batch, first=count):
            slab_copy(batch, first, i).start()
            return carry

        lax.fori_loop(0, batch[1] * batch[2], start, 0)
        count += batch[1] * batch[2]

    total[...] = jnp.zeros_like(total)
    own.wait()
    pl.semaphore_wait(barrier, 7)

    def piece(offset, part, half):
        return gathered.at[pl.ds(source(offset) * SHARD + part * (2 * PIECE) + half * PIECE, PIECE)]

    def wait_slot(t):
        rows = gathered.at[pl.ds(0, 6 * PIECE)]
        pltpu.make_async_remote_copy(
            rows, rows, sent_sem, slot_sem.at[t], device_id=(child, neighbour[0, 1]), device_id_type=MESH
        ).wait_recv()

    def multiply(number):
        batch, first = BATCHES[number], firsts[number]

        def one(i, carry):
            slab_copy(batch, first, i).wait()
            rows = pl.ds(pl.multiple_of(pair_of(batch, i) * PAIR, PAIR), PAIR)
            total[...] += jnp.dot(slab[first + i], gathered[rows, :], preferred_element_type=jnp.float32)
            return carry

        lax.fori_loop(0, batch[1] * batch[2], one, 0)

    def build(picker, length, column):
        def some(i, carry):
            rows = pl.ds(pl.multiple_of(i * 64, 64), 64)
            picker[rows, :] = jnp.where(column(rows, i), 1.0, 0.0).astype(jnp.bfloat16)
            return carry

        lax.fori_loop(0, length // 64, some, 0)

    def by_column(picker, table):
        width = picker.shape[1]
        build(
            picker,
            picker.shape[0],
            lambda rows, i: table[rows, :] == lax.broadcasted_iota(jnp.int32, (64, width), 1),
        )

    def by_row(picker, table):
        width = picker.shape[1]
        build(
            picker,
            picker.shape[0],
            lambda rows, i: table[...] == lax.broadcasted_iota(jnp.int32, (64, width), 0) + i * 64,
        )

    def own_rows():
        leaf = block.shape[1]
        rows = block.shape[0]
        for b in range(rows // leaf):
            value = jnp.dot(
                block[b * leaf : (b + 1) * leaf, :],
                parent_omega[b * leaf : (b + 1) * leaf, :],
                preferred_element_type=jnp.float32,
            )
            stacked[b * leaf : (b + 1) * leaf, :] = value[:, :128]
            stacked[rows + b * leaf : rows + (b + 1) * leaf, :] = value[:, 128:]

    slots, arrived = make_schedule(WINDOW)
    ready = [ready_slot(batch, arrived) for batch in BATCHES]
    done = 0
    for t in range(len(slots) + WINDOW):
        if t >= WINDOW:
            wait_slot(t - WINDOW)
        if t < len(slots):
            for link, offset, part, half in slots[t]:
                data = piece(offset, part, half)
                pltpu.make_async_remote_copy(
                    data, data, sent_sem, slot_sem.at[t], device_id=(child, neighbour[link]), device_id_type=MESH
                ).start()
        if t == 6:
            by_column(p1, t1)
        if t == 8:
            by_row(p2, t2)
        if t == 10:
            by_column(p3, t3)
        if t == 12:
            by_column(p4, t4)
        if t == 14:
            own_rows()
        while done < len(BATCHES) and ready[done] <= t - WINDOW:
            multiply(done)
            done += 1

    sent = gathered.at[pl.ds(0, 6 * PIECE * len(slots))]
    pltpu.make_async_remote_copy(
        sent, sent, sent_sem, slot_sem.at[0], device_id=(child, neighbour[0, 1]), device_id_type=MESH
    ).wait_send()

    pl.semaphore_signal(mate_sem, inc=1, device_id=(1 - child, chip), device_id_type=MESH)

    def fill(send, picker, height):
        def some(i, carry):
            rows = pl.ds(pl.multiple_of(i * 128, 128), 128)
            tiles = picked(picker[rows, :], parts[pl.ds(0, height), :]).reshape(128 // TILE, TILE, 128)
            send[pl.ds(pl.multiple_of(i * (128 // TILE), 128 // TILE), 128 // TILE)] = tiles
            return carry

        lax.fori_loop(0, OWNERS * TILE // 128, some, 0)

    def exchange(send, recv, sent_sem, came_sem):
        def one(step, carry):
            there = lax.rem(me + step, OWNERS)
            pltpu.make_async_remote_copy(
                send.at[there],
                recv.at[me],
                sent_sem,
                came_sem,
                device_id=(there // CHIPS, lax.rem(there, CHIPS)),
                device_id_type=MESH,
            ).start()
            return carry

        lax.fori_loop(1, OWNERS, one, 0)
        recv[me] = send[me]
        most = pl.ds(0, OWNERS - 1)
        everything = pltpu.make_async_remote_copy(
            send.at[most], recv.at[most], sent_sem, came_sem, device_id=(child, neighbour[0, 1]), device_id_type=MESH
        )
        everything.wait_recv()
        everything.wait_send()

    height = total.shape[0]
    parts[pl.ds(0, height), :] = two_parts(total[:, :128])
    parts[pl.ds(height, height), :] = two_parts(total[:, 128:])
    fill(send1, p1, 2 * height)
    pl.semaphore_wait(mate_sem, 1)
    exchange(send1, recv1, sent1, came1)
    parts[...] = two_parts(recv1[...].reshape(OWNERS * TILE, 128))
    rows = stacked.shape[0]

    def assemble(i, carry):
        some = pl.ds(pl.multiple_of(i * 128, 128), 128)
        stacked[some, :] += picked(p2[some, :], parts[...])
        return carry

    lax.fori_loop(0, rows // 128, assemble, 0)
    parts[pl.ds(0, rows), :] = two_parts(stacked[...])
    fill(send2, p3, rows)
    exchange(send2, recv2, sent2, came2)
    parts[...] = two_parts(recv2[...].reshape(OWNERS * TILE, 128))
    half = rows // 2
    for side in range(2):

        def finish(i, carry, side=side):
            some = pl.ds(pl.multiple_of(side * half + i * 128, 128), 128)
            out[pl.ds(pl.multiple_of(i * 128, 128), 128), side * 128 : (side + 1) * 128] = picked(p4[some, :], parts[...])
            return carry

        lax.fori_loop(0, half // 128, finish, 0)


def ranked(marked, values, capacity, empty):
    length = marked.shape[1]
    upto = jnp.tril(jnp.ones((length, length), jnp.bfloat16)).T
    rank = jnp.dot(marked.astype(jnp.bfloat16), upto, preferred_element_type=jnp.float32)
    rank = jnp.where(marked, rank.astype(jnp.int32), 0)
    kept = [
        jnp.sum(jnp.where(rank == k + 1, values - empty, 0), axis=1) + empty for k in range(capacity)
    ]
    return jnp.stack(kept, axis=1)


def both_halves(table, shift):
    other = jnp.where(table < 0, -1, table + shift)
    return jnp.concatenate([table, other, jnp.full((table.shape[0], 2), -1, jnp.int32)], axis=1)


def body(front_update, child_omega, parent_block, parent_omega, child_map, leaf_order):
    device_id = lax.axis_index("child") * CHIPS + lax.axis_index("rows")
    local_rows = front_update.shape[1]
    sample_cols = child_omega.shape[2]
    parent_dev = parent_block.shape[0]
    route = child_map.reshape(OWNERS, local_rows)
    mine = lax.dynamic_index_in_dim(route, device_id, 0, keepdims=False) // parent_dev
    to_owner = mine[None, :] == jnp.arange(OWNERS, dtype=jnp.int32)[:, None]
    t1 = ranked(to_owner, jnp.arange(local_rows, dtype=jnp.int32)[None, :], CAP, -1)
    t1 = both_halves(t1, local_rows).reshape(OWNERS * TILE, 1)
    t2 = ranked(route // parent_dev == device_id, route % parent_dev, CAP, -1)
    t2 = both_halves(t2, parent_dev).reshape(1, OWNERS * TILE)
    leaves = leaf_order.reshape(OWNERS, parent_dev)
    t3 = ranked(leaves // parent_dev == device_id, leaves % parent_dev, CAP, -1)
    t3 = both_halves(t3, parent_dev).reshape(OWNERS * TILE, 1)
    anchor = lax.dynamic_index_in_dim(leaves, device_id, 0, keepdims=False) // parent_dev
    where = jnp.arange(parent_dev, dtype=jnp.int32)
    before = (anchor[:, None] == anchor[None, :]) & (where[None, :] < where[:, None])
    t4 = anchor * TILE + jnp.sum(before.astype(jnp.int32), axis=1)
    t4 = jnp.concatenate([t4, t4 + CAP]).reshape(2 * parent_dev, 1)

    slots, _ = make_schedule(WINDOW)
    vmem = pl.BlockSpec(memory_space=pltpu.VMEM)
    anywhere = pl.BlockSpec(memory_space=pl.ANY)
    tiles = pltpu.VMEM((OWNERS, TILE, 128), jnp.float32)
    slot_rows = OWNERS * TILE
    dma = pltpu.SemaphoreType.DMA
    return pl.pallas_call(
        kernel,
        out_shape=jax.ShapeDtypeStruct((parent_dev, sample_cols), jnp.float32),
        in_specs=[anywhere, anywhere, vmem, vmem, vmem, vmem, vmem, vmem],
        out_specs=vmem,
        scratch_shapes=[
            pltpu.VMEM((CHIPS * SHARD, sample_cols), jnp.bfloat16),
            pltpu.VMEM((CHIPS // 2, local_rows, PAIR), jnp.bfloat16),
            pltpu.VMEM((local_rows, sample_cols), jnp.float32),
            pltpu.VMEM((2 * parent_dev, 128), jnp.float32),
            pltpu.VMEM((slot_rows, 256), jnp.bfloat16),
            tiles,
            tiles,
            tiles,
            tiles,
            pltpu.VMEM((slot_rows, 2 * local_rows), jnp.bfloat16),
            pltpu.VMEM((2 * parent_dev, slot_rows), jnp.bfloat16),
            pltpu.VMEM((slot_rows, 2 * parent_dev), jnp.bfloat16),
            pltpu.VMEM((2 * parent_dev, slot_rows), jnp.bfloat16),
            dma,
            dma((CHIPS // 2,)),
            dma,
            dma((len(slots),)),
            pltpu.SemaphoreType.REGULAR,
            dma,
            dma,
            dma,
            dma,
        ],
        compiler_params=pltpu.CompilerParams(
            collective_id=0, has_side_effects=True, vmem_limit_bytes=67043328
        ),
    )(front_update, child_omega, parent_block, parent_omega, t1, t2, t3, t4)


def solution(mesh):
    placed = (
        P("child", "rows", None),
        P("child", "rows", None),
        P(("child", "rows"), None),
        P(("child", "rows"), None),
        P(),
        P(),
    )
    return jax.shard_map(
        body, mesh=mesh, in_specs=placed, out_specs=P(("child", "rows"), None), check_vma=False
    )
```

time: 237 us -> 159 us (0.67)
  waiting for transfers between devices: 178 us -> 0 us
  Pallas kernels: 0 us -> 150 us
  matrix products: 23.5 us -> 1.17 us
  between operations: 13.6 us -> 0.13 us
  starting transfers between devices: 12.2 us -> 0 us
  other arithmetic: 4.4 us -> 0.4 us
  local copies, waits for them, and re-layouts: 4.57 us -> 7.8 us
    all_gather x1 -> x0, waiting for transfers between devices: 154 us -> none  [body(): lax.all_gather(child_omega, 'rows', axis=1, tiled=True)[0]]
    pallas_call x0 -> x1, Pallas kernels: none -> 150 us  [body(): pl.pallas_call(kernel, out_shape=jax.ShapeDtypeStruct((parent_dev, sample...]
    all_to_all x2 -> x0, waiting for transfers between devices: 23.1 us -> none  [the longest x1 11.8 us: body(): lax.all_to_all(sending.reshape(owners, leaf_capacity, sample_cols), ('chi...]
    dot_general x6 -> x0, matrix products: 22.8 us -> none  [the longest x1 19.9 us: body(): jnp.dot(slab_rows, lax.all_gather(child_omega, 'rows', axis=1, tiled=True...]
    all_to_all x2 -> x0, starting transfers between devices: 12.2 us -> none  [the longest x1 8.02 us: one_exchange(): lax.all_to_all(blocks, axis, split_axis=0, concat_axis=0, tiled=True)]
    reshape x5 -> x7, local copies, waits for them, and re-layouts: 2.39 us -> 5.65 us  [the longest x2 1.1 us: body(): route = child_map.reshape(OWNERS, local_rows)]
  transfers between devices with their start and end apart: 3 -> 0, of which waited for: 3 -> 0; matrix products, arithmetic and copies ran while one was open for 3% -> 0% of each run, Pallas kernels for 0% -> 0%
where the time goes in v2:
time: 159 us
  Pallas kernels  150 us (94%)
  local copies, waits for them, and re-layouts  7.8 us (5%)
    pallas_call x1, Pallas kernels, body(): pl.pallas_call(kernel, out_shape=jax.ShapeDtypeStruct((parent_dev, sample...  150 us

profile of v2, /device:TPU:1, one launch (start us, length us, event | category | flops | bytes accessed | tf_op | source)
XLA Modules:
  0.0 159.2 jit_solution(16610088679851008612)
XLA Ops:
  0.0 1.0 reshape.132
  1.0 0.1 copy.20
  1.1 0.3 select_reduce_fusion.3
  1.4 0.3 select_reduce_fusion.6
  1.9 0.1 copy.19
  2.0 0.1 copy.23
  2.1 0.7 reshape.134.t2
  2.8 1.0 reshape.135
  3.7 0.6 select_reduce_fusion
  4.5 0.2 convert_reduce_fusion
  4.7 0.1 copy.24
  4.8 0.9 reshape.140.t4
  5.7 1.0 reshape.139.t3
  6.7 1.0 reshape.138.t1
  7.7 149.7 %shard_map.64 = f32[384,256]{1,0:T(8,128)} custom-call(bf16[1,192,61440]{2,1,0:T(8,128)(2,1)} %front.1, bf16[1,960,256]{2,1,0:T(8,128)(2,1)} %omega.1, bf16[384,128]{1,0:T(8,128)(2,1)} %block.1, bf16[384,256]{1,0:T(8,128)(2,1)} %parent_omega.1, s32[1024,1]{1,0:T(8,128)} %reshape.138.t1, s32[1,1024]{1,0:T(1,128)} %reshape.134.t2, s32[1024,1]{1,0:T(8,128)} %reshape.139.t3, ...), custom_call_target="tpu_custom_call" | custom-call | tf_op jit(solution)/shard_map/pallas_call | solution.py:364
  157.4 1.8 %copy.29 = f32[384,256]{1,0:T(8,128)} copy(f32[384,256]{1,0:T(8,128)} %shard_map.64) | data formatting | bytes 786432
  (20 shorter events, 0.2 us)

commit v3 on v2

v3 whole, which is shorter than its diff:
```python
import functools

import jax
import jax.numpy as jnp
from jax import lax
from jax.experimental import pallas as pl
from jax.experimental.pallas import tpu as pltpu
from jax.sharding import PartitionSpec as P

MESH = pl.DeviceIdType.MESH
SIDE = 4
CHIPS = SIDE**3
OWNERS = 2 * CHIPS
SHARD = 960
PIECE = 160
PAIR = 2 * SHARD
CAP = 3
TILE = 8
WINDOW = 4
ORDERS = ((0, 1, 2), (1, 2, 0), (2, 0, 1))
BATCHES = (
    (0, 3, 3, 0, 0),
    (1, 3, 1, 0, 0),
    (1, 3, 1, 0, 1),
    (1, 3, 1, 0, 2),
    (0, 3, 1, 0, 3),
    (0, 1, 3, 3, 0),
    (1, 3, 1, 0, 3),
    (1, 1, 3, 3, 0),
    (0, 1, 1, 3, 3),
    (1, 1, 1, 3, 3),
)
WALK = (0, 1, 3, 2)


def moved(offset, dim, by):
    new = list(offset)
    new[dim] = (new[dim] + by) % SIDE
    return tuple(new)


def all_sends():
    sends = {(d, sign): [] for d in range(3) for sign in (1, -1)}
    for part, order in enumerate(ORDERS):
        for half, turn in enumerate((1, -1)):
            for phase in range(3):
                here = order[phase]
                for a in WALK:
                    for b in WALK:
                        inner = (a, b)
                        if any(inner[i] for i in range(2) if i >= phase):
                            continue
                        offset = [0, 0, 0]
                        for i in range(phase):
                            offset[order[i]] = inner[i]
                        for sign in (1, -1):
                            sends[here, sign].append((phase, 0, WALK.index(b), WALK.index(a), half, tuple(offset), part))
                        offset[here] = turn % SIDE
                        sends[here, turn].append((phase, 1, WALK.index(b), WALK.index(a), half, tuple(offset), part))
    return {link: sorted(found) for link, found in sends.items()}


def make_schedule(window):
    waiting = all_sends()
    links = list(waiting)
    arrived = {((0, 0, 0), part, half): -window for part in range(3) for half in range(2)}
    slots = []
    while any(waiting.values()):
        now, came = [], []
        for link in links:
            ready = [s for s in waiting[link] if arrived.get((s[5], s[6], s[4]), 10**6) + window <= len(slots)]
            assert ready
            chosen = ready[0]
            waiting[link].remove(chosen)
            now.append((link, chosen[5], chosen[6], chosen[4]))
            came.append((moved(chosen[5], *link), chosen[6], chosen[4]))
        for key in came:
            assert key not in arrived
            arrived[key] = len(slots)
        slots.append(now)
    return slots, arrived


def batch_members(batch):
    other, ny, nz, y0, z0 = batch
    return [(other, WALK[y0 + i % ny], WALK[z0 + i // ny]) for i in range(ny * nz)]


def ready_slot(batch, arrived):
    latest = 0
    for other, ry, rz in batch_members(batch):
        for rx in ((2, 1, 3) if other else (0, 1, 3)):
            for part in range(3):
                for half in range(2):
                    latest = max(latest, arrived[(rx, ry, rz), part, half])
    return latest


def two_parts(values):
    high = values.astype(jnp.bfloat16)
    low = (values - high.astype(jnp.float32)).astype(jnp.bfloat16)
    return jnp.concatenate([high, low], axis=-1)


def picked(picker, parts):
    both = jnp.dot(picker, parts, preferred_element_type=jnp.float32)
    return both[:, :128] + both[:, 128:]


def kernel(
    front, omega, block_in, parent_in, child_map, leaf_order, out_rows,
    gathered, slab, total, stacked, parts, send1, recv1, send2, recv2, p1, p2, p3, p4,
    block, parent_omega, map_rows, leaf_rows, map_table, columns, scratch,
    own_sem, slab_sem, in_sem, sent_sem, slot_sem, mate_sem, sent1, came1, sent2, came2,
):
    child = lax.axis_index("child")
    chip = lax.axis_index("rows")
    me = child * CHIPS + chip
    place = (lax.rem(chip, SIDE), lax.rem(chip // SIDE, SIDE), chip // (SIDE * SIDE))
    back = [[lax.rem(place[d] + SIDE - r, SIDE) for r in range(SIDE)] for d in range(3)]
    height = total.shape[0]
    rows = block.shape[0]

    def chip_at(xyz):
        return xyz[2] * (SIDE * SIDE) + xyz[1] * SIDE + xyz[0]

    def source(offset):
        return chip_at([back[d][offset[d]] for d in range(3)])

    neighbour = {}
    for d in range(3):
        for sign in (1, -1):
            offset = [0, 0, 0]
            offset[d] = -sign % SIDE
            neighbour[d, sign] = source(offset)

    own = pltpu.make_async_copy(omega.at[0], gathered.at[pl.ds(chip * SHARD, SHARD)], own_sem)
    own.start()
    barrier = pltpu.get_barrier_semaphore()
    for there in neighbour.values():
        pl.semaphore_signal(barrier, inc=1, device_id=(child, there), device_id_type=MESH)
    pl.semaphore_signal(barrier, inc=1, device_id=(1 - child, chip), device_id_type=MESH)

    def walk(i):
        return i + i // 2 - 2 * (i // 3)

    def pair_of(batch, i):
        other, ny, nz, y0, z0 = batch
        y = lax.rem(place[1] + SIDE - walk(y0 + lax.rem(i, ny)), SIDE)
        z = lax.rem(place[2] + SIDE - walk(z0 + i // ny), SIDE)
        half = place[0] // 2
        half = 1 - half if other else half
        return (z * SIDE + y) * 2 + half

    def slab_copy(batch, first, i):
        columns = pl.ds(pl.multiple_of(pair_of(batch, i) * PAIR, PAIR), PAIR)
        return pltpu.make_async_copy(front.at[0, :, columns], slab.at[first + i], slab_sem.at[first + i])

    firsts, count = [], 0
    for batch in BATCHES:
        firsts.append(count)
        count += batch[1] * batch[2]
    inputs = [
        pltpu.make_async_copy(source_ref, kept, in_sem.at[i])
        for i, (source_ref, kept) in enumerate(
            ((child_map, map_rows), (leaf_order, leaf_rows), (block_in, block), (parent_in, parent_omega))
        )
    ]

    def start_loads():
        for copy in inputs:
            copy.start()
        for batch, first in zip(BATCHES, firsts):

            def start(i, carry, batch=batch, first=first):
                slab_copy(batch, first, i).start()
                return carry

            lax.fori_loop(0, batch[1] * batch[2], start, 0)
        total[...] = jnp.zeros_like(total)

    def piece(offset, part, half):
        return gathered.at[pl.ds(source(offset) * SHARD + part * (2 * PIECE) + half * PIECE, PIECE)]

    def wait_slot(t):
        some = gathered.at[pl.ds(0, 6 * PIECE)]
        pltpu.make_async_remote_copy(
            some, some, sent_sem, slot_sem.at[t], device_id=(child, neighbour[0, 1]), device_id_type=MESH
        ).wait_recv()

    def multiply(number):
        batch, first = BATCHES[number], firsts[number]

        def one(i, carry):
            slab_copy(batch, first, i).wait()
            some = pl.ds(pl.multiple_of(pair_of(batch, i) * PAIR, PAIR), PAIR)
            total[...] += jnp.dot(slab[first + i], gathered[some, :], preferred_element_type=jnp.float32)
            return carry

        lax.fori_loop(0, batch[1] * batch[2], one, 0)

    def clear():
        recv1[...] = jnp.zeros_like(recv1)
        recv2[...] = jnp.zeros_like(recv2)

    def map_in():
        inputs[0].wait()
        for u in range(CHIPS // 2):
            for c in range(2):
                map_table[c * (CHIPS // 2) + u : c * (CHIPS // 2) + u + 1, :] = map_rows[
                    c : c + 1, u * 2 * height : (u + 1) * 2 * height
                ]

    def iota(shape, dim):
        return lax.broadcasted_iota(jnp.int32, shape, dim)

    def upto(n, segment):
        i, j = iota((n, n), 0), iota((n, n), 1)
        same = i <= j
        if segment < n:
            same = same & ((i >= segment) == (j >= segment))
        return jnp.where(same, 1.0, 0.0).astype(jnp.bfloat16)

    def prefix(marked, segment):
        ones = jnp.where(marked, 1.0, 0.0).astype(jnp.bfloat16)
        return jnp.dot(ones, upto(marked.shape[1], segment), preferred_element_type=jnp.float32)

    def find_places(values, segment):
        low = me * rows
        marked = (values >= low) & (values < low + rows)
        rank = prefix(marked, segment)
        local = (values - low + 1).astype(jnp.float32)
        n = values.shape[1]
        lane = iota(values.shape, 1)
        for e in range(n // segment):
            inside = marked & (lane >= e * segment) & (lane < (e + 1) * segment)
            for k in range(CAP):
                found = jnp.sum(jnp.where(inside & (rank == k + 1.0), local, 0.0), axis=1, keepdims=True) - 1.0
                columns[e * CAP + k, 0 : values.shape[0], :] = jnp.broadcast_to(found, (values.shape[0], 128))

    def place_rows(group, segments, width):
        def one(b, carry):
            index = group * 16 + b
            row = index // segments
            j = iota((TILE, 128), 0)
            lane = iota((TILE, 128), 1).astype(jnp.float32)
            kept = jnp.full((TILE, 128), -1.0, jnp.float32)
            for k in range(CAP):
                if segments == 1:
                    at = columns[k, pl.ds(row, 1), :]
                else:
                    odd = jnp.full((1, 128), lax.rem(index, 2), jnp.int32)
                    at = jnp.where(odd == 0, columns[k, pl.ds(row, 1), :], columns[CAP + k, pl.ds(row, 1), :])
                at = jnp.broadcast_to(at, (TILE, 128))
                kept = jnp.where(j == k, at, kept)
                shifted = at if width == rows else jnp.where(at < 0.0, -1.0, at + float(rows))
                kept = jnp.where(j == CAP + k, shifted, kept)
            for t in range(width // 128):
                scratch[pl.ds(pl.multiple_of(b * TILE, TILE), TILE), t * 128 : (t + 1) * 128] = jnp.where(
                    kept == lane + float(t * 128), 1.0, 0.0
                )
            return carry

        lax.fori_loop(0, 16, one, 0)

    def turn(picker, group):
        for t in range(2 * rows // 128):
            picker[t * 128 : (t + 1) * 128, pl.ds(pl.multiple_of(group * 128, 128), 128)] = jnp.transpose(
                scratch[:, t * 128 : (t + 1) * 128]
            ).astype(jnp.bfloat16)

    def over_groups(step):
        def one(group, carry):
            step(group)
            return carry

        return [lambda first=first: lax.fori_loop(first, first + 2, one, 0) for first in range(0, 8, 2)]

    def p2_group(group):
        place_rows(group, 2, 2 * rows)
        turn(p2, group)

    def p3_group(group):
        place_rows(group, 1, rows)
        p3[pl.ds(pl.multiple_of(group * 128, 128), 128), :] = scratch[:, 0:rows].astype(jnp.bfloat16)

    def codes(values, segment):
        n = values.shape[1]
        owner = iota((OWNERS, n), 0)
        spread = jnp.broadcast_to(values, (OWNERS, n))
        marked = (spread >= owner * rows) & (spread < owner * rows + rows)
        rank = prefix(marked, segment)
        code = (owner * TILE).astype(jnp.float32) + rank - 1.0
        return jnp.sum(jnp.where(marked, code, 0.0), axis=0, keepdims=True)

    def p1_all():
        both = codes(map_table[pl.ds(child * (CHIPS // 2) + chip // 2, 1), :], height)
        odd = jnp.full((1, height), lax.rem(chip, 2), jnp.int32)
        code = jnp.where(odd == 0, both[:, 0:height], both[:, height : 2 * height])

        def some(i, carry):
            slot = iota((128, height), 0)
            j = slot & (TILE - 1)
            wanted = jnp.where(j < CAP, slot, jnp.where(j < 2 * CAP, slot - CAP, -(10**6))) + i * 128
            p1[pl.ds(pl.multiple_of(i * 128, 128), 128), :] = jnp.where(
                wanted.astype(jnp.float32) == jnp.broadcast_to(code, (128, height)), 1.0, 0.0
            ).astype(jnp.bfloat16)
            return carry

        lax.fori_loop(0, OWNERS * TILE // 128, some, 0)

    def p4_codes():
        mine = [leaf_rows[pl.ds(me * CAP + c, 1), :] for c in range(CAP)]
        code = codes(jnp.concatenate(mine, axis=1), rows)
        columns[0, 0:CAP, :] = jnp.concatenate([code[:, c * 128 : (c + 1) * 128] for c in range(CAP)], axis=0)

    def p4_group(group):
        for t in range(2 * CAP):
            code = jnp.broadcast_to(columns[0, t % CAP : t % CAP + 1, :], (128, 128))
            slot = (iota((128, 128), 0) + group * 128 - (t // CAP) * CAP).astype(jnp.float32)
            scratch[:, t * 128 : (t + 1) * 128] = jnp.where(slot == code, 1.0, 0.0)
        turn(p4, group)

    def leaf_places():
        inputs[1].wait()
        find_places(
            jnp.concatenate([leaf_rows[pl.ds(c, OWNERS, stride=CAP), :] for c in range(CAP)], axis=1), rows
        )

    def own_rows():
        inputs[2].wait()
        inputs[3].wait()
        leaf = block.shape[1]
        for b in range(rows // leaf):
            value = jnp.dot(
                block[b * leaf : (b + 1) * leaf, :],
                parent_omega[b * leaf : (b + 1) * leaf, :],
                preferred_element_type=jnp.float32,
            )
            stacked[b * leaf : (b + 1) * leaf, :] = value[:, :128]
            stacked[rows + b * leaf : rows + (b + 1) * leaf, :] = value[:, 128:]

    jobs = [start_loads, clear, map_in, lambda: find_places(map_table[...], height)]
    jobs += over_groups(p2_group)
    jobs += [p1_all, leaf_places]
    jobs += over_groups(p3_group)
    jobs += [p4_codes]
    jobs += over_groups(p4_group)
    jobs += [own_rows]

    own.wait()
    pl.semaphore_wait(barrier, 7)
    slots, arrived = make_schedule(WINDOW)
    ready = [ready_slot(batch, arrived) for batch in BATCHES]
    done = 0
    for t in range(len(slots) + WINDOW):
        if t >= WINDOW:
            wait_slot(t - WINDOW)
        if t < len(slots):
            for link, offset, part, half in slots[t]:
                data = piece(offset, part, half)
                pltpu.make_async_remote_copy(
                    data, data, sent_sem, slot_sem.at[t], device_id=(child, neighbour[link]), device_id_type=MESH
                ).start()
        if t >= WINDOW - 1 and jobs:
            jobs.pop(0)()
        if t == len(slots) + WINDOW - 1:
            pl.semaphore_signal(mate_sem, inc=1, device_id=(1 - child, chip), device_id_type=MESH)
        while done < len(BATCHES) and ready[done] <= t - WINDOW:
            multiply(done)
            done += 1

    def fill(send, picker, values):
        n = values.shape[1]

        def some(i, carry):
            both = jnp.dot(
                picker[pl.ds(pl.multiple_of(i * 512, 512), 512), :], values, preferred_element_type=jnp.float32
            )
            left = iota((512, 128), 0) & (TILE - 1)
            tile = jnp.where(left < CAP, both[:, 0:128] + both[:, 128:256], both[:, 256:384] + both[:, 384:512])
            send[pl.ds(pl.multiple_of(i * (512 // TILE), 512 // TILE), 512 // TILE)] = tile.reshape(512 // TILE, TILE, 128)
            return carry

        lax.fori_loop(0, OWNERS * TILE // 512, some, 0)

    used = pl.ds(0, 2 * CAP)

    def exchange(send, recv, sent_sem, came_sem):
        order = []
        for dx in range(SIDE):
            for dy in range(SIDE):
                for dz in range(SIDE):
                    for other in range(2):
                        far = sum(min(v, SIDE - v) for v in (dx, dy, dz))
                        if far or other:
                            order.append((-far, dx, dy, dz, other))
        for _, dx, dy, dz, other in sorted(order):
            to = source((dx, dy, dz))
            kid = 1 - child if other else child
            pltpu.make_async_remote_copy(
                send.at[kid * CHIPS + to, used],
                recv.at[me, used],
                sent_sem,
                came_sem,
                device_id=(kid, to),
                device_id_type=MESH,
            ).start()
        recv[me] = send[me]
        most = pl.ds(0, OWNERS - 1)
        everything = pltpu.make_async_remote_copy(
            send.at[most, used],
            recv.at[most, used],
            sent_sem,
            came_sem,
            device_id=(child, neighbour[0, 1]),
            device_id_type=MESH,
        )
        everything.wait_recv()
        return everything

    fill(send1, p1, jnp.concatenate([two_parts(total[:, :128]), two_parts(total[:, 128:])], axis=1))
    pl.semaphore_wait(mate_sem, 1)
    first = exchange(send1, recv1, sent1, came1)
    parts[...] = two_parts(recv1[...].reshape(OWNERS * TILE, 128))
    for side in range(2):
        stacked[side * rows : (side + 1) * rows, :] += picked(p2[side * rows : (side + 1) * rows, :], parts[...])
    fill(send2, p3, jnp.concatenate([two_parts(stacked[0:rows, :]), two_parts(stacked[rows : 2 * rows, :])], axis=1))
    second = exchange(send2, recv2, sent2, came2)
    parts[...] = two_parts(recv2[...].reshape(OWNERS * TILE, 128))
    for side in range(2):
        out_rows[:, side * 128 : (side + 1) * 128] = picked(p4[side * rows : (side + 1) * rows, :], parts[...])
    first.wait_send()
    second.wait_send()
    sent = gathered.at[pl.ds(0, 6 * PIECE * len(slots))]
    pltpu.make_async_remote_copy(
        sent, sent, sent_sem, slot_sem.at[0], device_id=(child, neighbour[0, 1]), device_id_type=MESH
    ).wait_send()


def body(front_update, child_omega, parent_block, parent_omega, child_map, leaf_order):
    local_rows = front_update.shape[1]
    sample_cols = child_omega.shape[2]
    parent_dev, leaf_size = parent_block.shape
    slots, _ = make_schedule(WINDOW)
    vmem = pl.BlockSpec(memory_space=pltpu.VMEM)
    anywhere = pl.BlockSpec(memory_space=pl.ANY)
    tiles = pltpu.VMEM((OWNERS, TILE, 128), jnp.float32)
    slot_rows = OWNERS * TILE
    dma = pltpu.SemaphoreType.DMA
    result = pl.pallas_call(
        kernel,
        out_shape=jax.ShapeDtypeStruct((parent_dev, sample_cols), jnp.float32),
        in_specs=[anywhere] * 6,
        out_specs=vmem,
        scratch_shapes=[
            pltpu.VMEM((CHIPS * SHARD, sample_cols), jnp.bfloat16),
            pltpu.VMEM((CHIPS // 2, local_rows, PAIR), jnp.bfloat16),
            pltpu.VMEM((local_rows, sample_cols), jnp.float32),
            pltpu.VMEM((2 * parent_dev, 128), jnp.float32),
            pltpu.VMEM((slot_rows, 256), jnp.bfloat16),
            tiles,
            tiles,
            tiles,
            tiles,
            pltpu.VMEM((slot_rows, local_rows), jnp.bfloat16),
            pltpu.VMEM((2 * parent_dev, slot_rows), jnp.bfloat16),
            pltpu.VMEM((slot_rows, parent_dev), jnp.bfloat16),
            pltpu.VMEM((2 * parent_dev, slot_rows), jnp.bfloat16),
            pltpu.VMEM((parent_dev, leaf_size), jnp.bfloat16),
            pltpu.VMEM((parent_dev, sample_cols), jnp.bfloat16),
            pltpu.VMEM(child_map.shape, jnp.int32),
            pltpu.VMEM((parent_dev, 128), jnp.int32),
            pltpu.VMEM((OWNERS // 2, 2 * local_rows), jnp.int32),
            pltpu.VMEM((2 * CAP, OWNERS, 128), jnp.float32),
            pltpu.VMEM((128, 2 * parent_dev), jnp.float32),
            dma,
            dma((CHIPS // 2,)),
            dma((4,)),
            dma,
            dma((len(slots),)),
            pltpu.SemaphoreType.REGULAR,
            dma,
            dma,
            dma,
            dma,
        ],
        compiler_params=pltpu.CompilerParams(
            collective_id=0, has_side_effects=True, vmem_limit_bytes=67043328
        ),
    )(front_update, child_omega, parent_block, parent_omega, child_map, leaf_order.reshape(parent_dev, 128))
    return result


def solution(mesh):
    placed = (
        P("child", "rows", None),
        P("child", "rows", None),
        P(("child", "rows"), None),
        P(("child", "rows"), None),
        P(),
        P(),
    )
    return jax.shard_map(
        body, mesh=mesh, in_specs=placed, out_specs=P(("child", "rows"), None), check_vma=False
    )
```

time: 159 us -> 144 us (0.906)
  Pallas kernels: 150 us -> 142 us
  local copies, waits for them, and re-layouts: 7.8 us -> 1.77 us
    pallas_call x1, Pallas kernels: 150 us -> 142 us  [body(): pl.pallas_call(kernel, out_shape=jax.ShapeDtypeStruct((parent_dev, sample...]
    reshape x7 -> x0, local copies, waits for them, and re-layouts: 5.65 us -> none  [the longest x2 1.1 us: body(): route = child_map.reshape(OWNERS, local_rows)]
where the time goes in v3:
time: 144 us
  Pallas kernels  142 us (99%)
  local copies, waits for them, and re-layouts  1.77 us (1%)
    pallas_call x1, Pallas kernels, body(): pl.pallas_call(kernel, out_shape=jax.ShapeDtypeStruct((parent_dev, sample...  142 us

profile of v3, /device:TPU:1, one launch (start us, length us, event | category | flops | bytes accessed | tf_op | source)
XLA Modules:
  0.0 144.3 jit_solution(7420464728521534808)
XLA Ops:
  0.0 142.5 %shard_map.64 = f32[384,256]{1,0:T(8,128)} custom-call(bf16[1,192,61440]{2,1,0:T(8,128)(2,1)} %front.1, bf16[1,960,256]{2,1,0:T(8,128)(2,1)} %omega.1, bf16[384,128]{1,0:T(8,128)(2,1)} %block_in.1, bf16[384,256]{1,0:T(8,128)(2,1)} %parent_in.1, s32[2,12288]{1,0:T(2,128)} %child_map.1, s32[384,128]{1,0:T(8,128)} %bitcast.1), custom_call_target="tpu_custom_call" | custom-call | tf_op jit(solution)/shard_map/pallas_call | solution.py:451
  142.5 1.8 %copy.8 = f32[384,256]{1,0:T(8,128)} copy(f32[384,256]{1,0:T(8,128)} %shard_map.64) | data formatting | bytes 786432

commit v4 on v3

--- a/solution.py
+++ b/solution.py
@@ -25,8 +25,10 @@
     (1, 3, 1, 0, 2),
     (0, 3, 1, 0, 3),
     (0, 1, 3, 3, 0),
-    (1, 3, 1, 0, 3),
-    (1, 1, 3, 3, 0),
+    (1, 2, 1, 0, 3),
+    (1, 1, 2, 3, 0),
+    (1, 1, 1, 2, 3),
+    (1, 1, 1, 3, 2),
     (0, 1, 1, 3, 3),
     (1, 1, 1, 3, 3),
 )
@@ -238,7 +240,7 @@
                 found = jnp.sum(jnp.where(inside & (rank == k + 1.0), local, 0.0), axis=1, keepdims=True) - 1.0
                 columns[e * CAP + k, 0 : values.shape[0], :] = jnp.broadcast_to(found, (values.shape[0], 128))
 
-    def place_rows(group, segments, width):
+    def place_rows(group, segments):
         def one(b, carry):
             index = group * 16 + b
             row = index // segments
@@ -251,11 +253,8 @@
                 else:
                     odd = jnp.full((1, 128), lax.rem(index, 2), jnp.int32)
                     at = jnp.where(odd == 0, columns[k, pl.ds(row, 1), :], columns[CAP + k, pl.ds(row, 1), :])
-                at = jnp.broadcast_to(at, (TILE, 128))
-                kept = jnp.where(j == k, at, kept)
-                shifted = at if width == rows else jnp.where(at < 0.0, -1.0, at + float(rows))
-                kept = jnp.where(j == CAP + k, shifted, kept)
-            for t in range(width // 128):
+                kept = jnp.where(j == k, jnp.broadcast_to(at, (TILE, 128)), kept)
+            for t in range(rows // 128):
                 scratch[pl.ds(pl.multiple_of(b * TILE, TILE), TILE), t * 128 : (t + 1) * 128] = jnp.where(
                     kept == lane + float(t * 128), 1.0, 0.0
                 )
@@ -264,7 +263,7 @@
         lax.fori_loop(0, 16, one, 0)
 
     def turn(picker, group):
-        for t in range(2 * rows // 128):
+        for t in range(rows // 128):
             picker[t * 128 : (t + 1) * 128, pl.ds(pl.multiple_of(group * 128, 128), 128)] = jnp.transpose(
                 scratch[:, t * 128 : (t + 1) * 128]
             ).astype(jnp.bfloat16)
@@ -277,12 +276,12 @@
         return [lambda first=first: lax.fori_loop(first, first + 2, one, 0) for first in range(0, 8, 2)]
 
     def p2_group(group):
-        place_rows(group, 2, 2 * rows)
+        place_rows(group, 2)
         turn(p2, group)
 
     def p3_group(group):
-        place_rows(group, 1, rows)
-        p3[pl.ds(pl.multiple_of(group * 128, 128), 128), :] = scratch[:, 0:rows].astype(jnp.bfloat16)
+        place_rows(group, 1)
+        p3[pl.ds(pl.multiple_of(group * 128, 128), 128), :] = scratch[...].astype(jnp.bfloat16)
 
     def codes(values, segment):
         n = values.shape[1]
@@ -301,7 +300,7 @@
         def some(i, carry):
             slot = iota((128, height), 0)
             j = slot & (TILE - 1)
-            wanted = jnp.where(j < CAP, slot, jnp.where(j < 2 * CAP, slot - CAP, -(10**6))) + i * 128
+            wanted = jnp.where(j < CAP, slot, -(10**6)) + i * 128
             p1[pl.ds(pl.multiple_of(i * 128, 128), 128), :] = jnp.where(
                 wanted.astype(jnp.float32) == jnp.broadcast_to(code, (128, height)), 1.0, 0.0
             ).astype(jnp.bfloat16)
@@ -315,9 +314,9 @@
         columns[0, 0:CAP, :] = jnp.concatenate([code[:, c * 128 : (c + 1) * 128] for c in range(CAP)], axis=0)
 
     def p4_group(group):
-        for t in range(2 * CAP):
-            code = jnp.broadcast_to(columns[0, t % CAP : t % CAP + 1, :], (128, 128))
-            slot = (iota((128, 128), 0) + group * 128 - (t // CAP) * CAP).astype(jnp.float32)
+        for t in range(CAP):
+            code = jnp.broadcast_to(columns[0, t : t + 1, :], (128, 128))
+            slot = (iota((128, 128), 0) + group * 128).astype(jnp.float32)
             scratch[:, t * 128 : (t + 1) * 128] = jnp.where(slot == code, 1.0, 0.0)
         turn(p4, group)
 
@@ -371,31 +370,28 @@
             done += 1
 
     def fill(send, picker, values):
-        n = values.shape[1]
+        both = two_parts(values)
 
         def some(i, carry):
-            both = jnp.dot(
-                picker[pl.ds(pl.multiple_of(i * 512, 512), 512), :], values, preferred_element_type=jnp.float32
-            )
-            left = iota((512, 128), 0) & (TILE - 1)
-            tile = jnp.where(left < CAP, both[:, 0:128] + both[:, 128:256], both[:, 256:384] + both[:, 384:512])
+            tile = picked(picker[pl.ds(pl.multiple_of(i * 512, 512), 512), :], both)
             send[pl.ds(pl.multiple_of(i * (512 // TILE), 512 // TILE), 512 // TILE)] = tile.reshape(512 // TILE, TILE, 128)
             return carry
 
         lax.fori_loop(0, OWNERS * TILE // 512, some, 0)
 
-    used = pl.ds(0, 2 * CAP)
+    used = pl.ds(0, CAP)
+    order = []
+    for dx in range(SIDE):
+        for dy in range(SIDE):
+            for dz in range(SIDE):
+                for other in range(2):
+                    far = sum(min(v, SIDE - v) for v in (dx, dy, dz))
+                    if far or other:
+                        order.append((-far, dx, dy, dz, other))
+    order.sort()
 
     def exchange(send, recv, sent_sem, came_sem):
-        order = []
-        for dx in range(SIDE):
-            for dy in range(SIDE):
-                for dz in range(SIDE):
-                    for other in range(2):
-                        far = sum(min(v, SIDE - v) for v in (dx, dy, dz))
-                        if far or other:
-                            order.append((-far, dx, dy, dz, other))
-        for _, dx, dy, dz, other in sorted(order):
+        for _, dx, dy, dz, other in order:
             to = source((dx, dy, dz))
             kid = 1 - child if other else child
             pltpu.make_async_remote_copy(
@@ -408,7 +404,7 @@
             ).start()
         recv[me] = send[me]
         most = pl.ds(0, OWNERS - 1)
-        everything = pltpu.make_async_remote_copy(
+        return pltpu.make_async_remote_copy(
             send.at[most, used],
             recv.at[most, used],
             sent_sem,
@@ -416,22 +412,27 @@
             device_id=(child, neighbour[0, 1]),
             device_id_type=MESH,
         )
-        everything.wait_recv()
-        return everything
-
-    fill(send1, p1, jnp.concatenate([two_parts(total[:, :128]), two_parts(total[:, 128:])], axis=1))
-    pl.semaphore_wait(mate_sem, 1)
-    first = exchange(send1, recv1, sent1, came1)
-    parts[...] = two_parts(recv1[...].reshape(OWNERS * TILE, 128))
+
+    def here(side):
+        return slice(side * rows, (side + 1) * rows)
+
+    first, second = [], []
     for side in range(2):
-        stacked[side * rows : (side + 1) * rows, :] += picked(p2[side * rows : (side + 1) * rows, :], parts[...])
-    fill(send2, p3, jnp.concatenate([two_parts(stacked[0:rows, :]), two_parts(stacked[rows : 2 * rows, :])], axis=1))
-    second = exchange(send2, recv2, sent2, came2)
-    parts[...] = two_parts(recv2[...].reshape(OWNERS * TILE, 128))
+        fill(send1.at[side], p1, total[:, side * 128 : (side + 1) * 128])
+        if side == 0:
+            pl.semaphore_wait(mate_sem, 1)
+        first.append(exchange(send1.at[side], recv1.at[side], sent1.at[side], came1.at[side]))
     for side in range(2):
-        out_rows[:, side * 128 : (side + 1) * 128] = picked(p4[side * rows : (side + 1) * rows, :], parts[...])
-    first.wait_send()
-    second.wait_send()
+        first[side].wait_recv()
+        parts[...] = two_parts(recv1[side].reshape(OWNERS * TILE, 128))
+        fill(send2.at[side], p3, stacked[here(side), :] + picked(p2[...], parts[...]))
+        second.append(exchange(send2.at[side], recv2.at[side], sent2.at[side], came2.at[side]))
+    for side in range(2):
+        second[side].wait_recv()
+        parts[...] = two_parts(recv2[side].reshape(OWNERS * TILE, 128))
+        out_rows[here(side), :] = picked(p4[...], parts[...])
+    for copy in first + second:
+        copy.wait_send()
     sent = gathered.at[pl.ds(0, 6 * PIECE * len(slots))]
     pltpu.make_async_remote_copy(
         sent, sent, sent_sem, slot_sem.at[0], device_id=(child, neighbour[0, 1]), device_id_type=MESH
@@ -445,12 +446,12 @@
     slots, _ = make_schedule(WINDOW)
     vmem = pl.BlockSpec(memory_space=pltpu.VMEM)
     anywhere = pl.BlockSpec(memory_space=pl.ANY)
-    tiles = pltpu.VMEM((OWNERS, TILE, 128), jnp.float32)
+    tiles = pltpu.VMEM((2, OWNERS, TILE, 128), jnp.float32)
     slot_rows = OWNERS * TILE
     dma = pltpu.SemaphoreType.DMA
     result = pl.pallas_call(
         kernel,
-        out_shape=jax.ShapeDtypeStruct((parent_dev, sample_cols), jnp.float32),
+        out_shape=jax.ShapeDtypeStruct((2 * parent_dev, 128), jnp.float32),
         in_specs=[anywhere] * 6,
         out_specs=vmem,
         scratch_shapes=[
@@ -464,32 +465,32 @@
             tiles,
             tiles,
             pltpu.VMEM((slot_rows, local_rows), jnp.bfloat16),
-            pltpu.VMEM((2 * parent_dev, slot_rows), jnp.bfloat16),
+            pltpu.VMEM((parent_dev, slot_rows), jnp.bfloat16),
             pltpu.VMEM((slot_rows, parent_dev), jnp.bfloat16),
-            pltpu.VMEM((2 * parent_dev, slot_rows), jnp.bfloat16),
+            pltpu.VMEM((parent_dev, slot_rows), jnp.bfloat16),
             pltpu.VMEM((parent_dev, leaf_size), jnp.bfloat16),
             pltpu.VMEM((parent_dev, sample_cols), jnp.bfloat16),
             pltpu.VMEM(child_map.shape, jnp.int32),
             pltpu.VMEM((parent_dev, 128), jnp.int32),
             pltpu.VMEM((OWNERS // 2, 2 * local_rows), jnp.int32),
             pltpu.VMEM((2 * CAP, OWNERS, 128), jnp.float32),
-            pltpu.VMEM((128, 2 * parent_dev), jnp.float32),
+            pltpu.VMEM((128, parent_dev), jnp.float32),
             dma,
             dma((CHIPS // 2,)),
             dma((4,)),
             dma,
             dma((len(slots),)),
             pltpu.SemaphoreType.REGULAR,
-            dma,
-            dma,
-            dma,
-            dma,
+            dma((2,)),
+            dma((2,)),
+            dma((2,)),
+            dma((2,)),
         ],
         compiler_params=pltpu.CompilerParams(
             collective_id=0, has_side_effects=True, vmem_limit_bytes=67043328
         ),
     )(front_update, child_omega, parent_block, parent_omega, child_map, leaf_order.reshape(parent_dev, 128))
-    return result
+    return jnp.concatenate([result[:parent_dev], result[parent_dev:]], axis=1)
 
 
 def solution(mesh):

time: 144 us -> 142 us (0.986)
  Pallas kernels: 142 us -> 140 us
    pallas_call x1, Pallas kernels: 142 us -> 140 us  [body(): pl.pallas_call(kernel, out_shape=jax.ShapeDtypeStruct((2 * parent_dev, 12...]
    unnamed x1 -> x0, local copies, waits for them, and re-layouts: 1.77 us -> none
where the time goes in v4:
time: 142 us
  Pallas kernels  140 us (99%)
    pallas_call x1, Pallas kernels, body(): pl.pallas_call(kernel, out_shape=jax.ShapeDtypeStruct((2 * parent_dev, 12...  140 us

profile of v4, /device:TPU:1, one launch (start us, length us, event | category | flops | bytes accessed | tf_op | source)
XLA Modules:
  0.0 141.9 jit_solution(7754235341346956215)
XLA Ops:
  0.0 140.1 %shard_map.64 = f32[768,128]{1,0:T(8,128)} custom-call(bf16[1,192,61440]{2,1,0:T(8,128)(2,1)} %front.1, bf16[1,960,256]{2,1,0:T(8,128)(2,1)} %omega.1, bf16[384,128]{1,0:T(8,128)(2,1)} %block_in.1, bf16[384,256]{1,0:T(8,128)(2,1)} %parent_in.1, s32[2,12288]{1,0:T(2,128)} %child_map.1, s32[384,128]{1,0:T(8,128)} %bitcast.1), custom_call_target="tpu_custom_call" | custom-call | tf_op jit(solution)/shard_map/pallas_call | solution.py:452
  140.1 1.0 fusion
  141.1 0.8 pad_maximum_fusion

commit v5 on v4

--- a/solution.py
+++ b/solution.py
@@ -12,90 +12,113 @@
 CHIPS = SIDE**3
 OWNERS = 2 * CHIPS
 SHARD = 960
-PIECE = 160
+THIRD = 256
+REST = SHARD - 3 * THIRD
 PAIR = 2 * SHARD
 CAP = 3
 TILE = 8
 WINDOW = 4
-ORDERS = ((0, 1, 2), (1, 2, 0), (2, 0, 1))
-BATCHES = (
-    (0, 3, 3, 0, 0),
-    (1, 3, 1, 0, 0),
-    (1, 3, 1, 0, 1),
-    (1, 3, 1, 0, 2),
-    (0, 3, 1, 0, 3),
-    (0, 1, 3, 3, 0),
-    (1, 2, 1, 0, 3),
-    (1, 1, 2, 3, 0),
-    (1, 1, 1, 2, 3),
-    (1, 1, 1, 3, 2),
-    (0, 1, 1, 3, 3),
-    (1, 1, 1, 3, 3),
-)
-WALK = (0, 1, 3, 2)
-
-
-def moved(offset, dim, by):
-    new = list(offset)
-    new[dim] = (new[dim] + by) % SIDE
-    return tuple(new)
+UNIT = 64
+STEP = 2
+
+
+def drop_bit(r, d):
+    return ((r >> (d + 1)) << d) | (r & ((1 << d) - 1))
+
+
+def chunk_sets():
+    found = []
+    for d in range(3):
+        e, f = (d + 1) % 3, (d + 2) % 3
+        for h, links in enumerate(((e, 3 + d, f, 3 + e, 3 + f), (f, 3 + d, e, 3 + f, 3 + e))):
+            found.append((("T", d, h), links, (0.0, 1.0, 2.0, 3.0, 4.0), 2))
+    for i in range(3):
+        b, c = (i + 1) % 3, (i + 2) % 3
+        found.append((("R", i, 0), (i, b, 3 + i, 3 + b, c, 3 + c), (0.5, 1.5, 2.5, 3.5, 3.7, 9.0), 1))
+    return found
 
 
 def all_sends():
-    sends = {(d, sign): [] for d in range(3) for sign in (1, -1)}
-    for part, order in enumerate(ORDERS):
-        for half, turn in enumerate((1, -1)):
-            for phase in range(3):
-                here = order[phase]
-                for a in WALK:
-                    for b in WALK:
-                        inner = (a, b)
-                        if any(inner[i] for i in range(2) if i >= phase):
-                            continue
-                        offset = [0, 0, 0]
-                        for i in range(phase):
-                            offset[order[i]] = inner[i]
-                        for sign in (1, -1):
-                            sends[here, sign].append((phase, 0, WALK.index(b), WALK.index(a), half, tuple(offset), part))
-                        offset[here] = turn % SIDE
-                        sends[here, turn].append((phase, 1, WALK.index(b), WALK.index(a), half, tuple(offset), part))
-    return {link: sorted(found) for link, found in sends.items()}
+    sends = [[] for _ in range(6)]
+    for name, links, ranks, size in chunk_sets():
+        held = [0]
+        for link, rank in zip(links, ranks):
+            for r in held:
+                order = (bin(r >> 3).count("1"), r >> 3, r) if rank == 9.0 else (0, 0, 0)
+                sends[link].append((rank, order, name, r, size))
+            held = held + [r ^ (1 << link) for r in held]
+    for d in range(3):
+        for r in range(CHIPS):
+            if (r >> d) & 1:
+                sends[d].append((5.0, (0, 0, drop_bit(r, d)), ("F", d, 0), r, 3))
+        sends[d].append((6.0, (0, 0, 0), ("S", d, 0), 0, 6))
+    return [sorted(found) for found in sends]
+
+
+def loaded_step(r):
+    return 3 + r // 16
+
+
+T_BATCHES = tuple((d, 8 * g, 8) for g in range(4) for d in range(3))
+R_BATCHES = tuple((4 * m, 4) for m in (0, 1, 2, 4, 3, 5, 6)) + tuple((28 + i, 1) for i in range(4))
+
+
+def insert_bit(idx, d):
+    return ((idx >> d) << (d + 1)) | (idx & ((1 << d) - 1))
+
+
+def t_ready(batch, arrived):
+    d, first, count = batch
+    latest = 0
+    for idx in range(first, first + count):
+        r = insert_bit(idx, d)
+        for key in ((("T", d, 0), r), (("T", d, 1), r), (("F", d, 0), r)):
+            latest = max(latest, arrived.get(key, 10**6))
+    return latest
+
+
+def r_ready(batch, arrived):
+    first, count = batch
+    return max(arrived.get((("R", i, 0), r), 10**6) for i in range(3) for r in range(2 * first, 2 * (first + count)))
 
 
 def make_schedule(window):
     waiting = all_sends()
-    links = list(waiting)
-    arrived = {((0, 0, 0), part, half): -window for part in range(3) for half in range(2)}
-    slots = []
-    while any(waiting.values()):
+    arrived = {(name, 0): -window for name, _, _, _ in chunk_sets()}
+    free = [0] * 6
+    steps = []
+    while any(waiting):
+        t = len(steps)
         now, came = [], []
-        for link in links:
-            ready = [s for s in waiting[link] if arrived.get((s[5], s[6], s[4]), 10**6) + window <= len(slots)]
-            assert ready
-            chosen = ready[0]
-            waiting[link].remove(chosen)
-            now.append((link, chosen[5], chosen[6], chosen[4]))
-            came.append((moved(chosen[5], *link), chosen[6], chosen[4]))
+        for link in range(6):
+            free[link] = max(free[link], STEP * t)
+            while free[link] < STEP * (t + 1):
+                chosen = None
+                for item in waiting[link]:
+                    _, _, name, r, size = item
+                    if name[0] == "F":
+                        fit = loaded_step(r) <= t
+                    elif name[0] == "S":
+                        last = max(t_ready(b, arrived) for b in T_BATCHES if b[0] == name[1])
+                        fit = last + window + 1 <= t
+                    else:
+                        fit = arrived.get((name, r), 10**6) + window <= t
+                    if fit:
+                        chosen = item
+                        break
+                if chosen is None:
+                    break
+                waiting[link].remove(chosen)
+                _, _, name, r, size = chosen
+                free[link] += size
+                now.append((link, name, r, size))
+                came.append((name, r ^ (1 << link)))
         for key in came:
             assert key not in arrived
-            arrived[key] = len(slots)
-        slots.append(now)
-    return slots, arrived
-
-
-def batch_members(batch):
-    other, ny, nz, y0, z0 = batch
-    return [(other, WALK[y0 + i % ny], WALK[z0 + i // ny]) for i in range(ny * nz)]
-
-
-def ready_slot(batch, arrived):
-    latest = 0
-    for other, ry, rz in batch_members(batch):
-        for rx in ((2, 1, 3) if other else (0, 1, 3)):
-            for part in range(3):
-                for half in range(2):
-                    latest = max(latest, arrived[(rx, ry, rz), part, half])
-    return latest
+            arrived[key] = t
+        steps.append(now)
+        assert t < 200
+    return steps, arrived
 
 
 def two_parts(values):
@@ -111,57 +134,81 @@
 
 def kernel(
     front, omega, block_in, parent_in, child_map, leaf_order, out_rows,
-    gathered, slab, total, stacked, parts, send1, recv1, send2, recv2, p1, p2, p3, p4,
+    thirds, rests, slab_t, slab_r, lent, total, partial, came, stacked, parts, send1, recv1, send2, recv2, p1, p2, p3, p4,
     block, parent_omega, map_rows, leaf_rows, map_table, columns, scratch,
-    own_sem, slab_sem, in_sem, sent_sem, slot_sem, mate_sem, sent1, came1, sent2, came2,
+    own_sem, t_sem, r_sem, in_sem, sent_sem, slot_sem, mate_sem, sent1, came1, sent2, came2,
 ):
     child = lax.axis_index("child")
     chip = lax.axis_index("rows")
     me = child * CHIPS + chip
     place = (lax.rem(chip, SIDE), lax.rem(chip // SIDE, SIDE), chip // (SIDE * SIDE))
-    back = [[lax.rem(place[d] + SIDE - r, SIDE) for r in range(SIDE)] for d in range(3)]
+    back = []
+    for d in range(3):
+        v = place[d]
+        flipped = v + 1 - 2 * lax.rem(v, 2)
+        back.append([v, flipped, 3 - v, 3 - flipped])
+    odd = lax.rem(place[0], 2)
     height = total.shape[0]
     rows = block.shape[0]
 
     def chip_at(xyz):
         return xyz[2] * (SIDE * SIDE) + xyz[1] * SIDE + xyz[0]
 
-    def source(offset):
-        return chip_at([back[d][offset[d]] for d in range(3)])
-
-    neighbour = {}
-    for d in range(3):
-        for sign in (1, -1):
-            offset = [0, 0, 0]
-            offset[d] = -sign % SIDE
-            neighbour[d, sign] = source(offset)
-
-    own = pltpu.make_async_copy(omega.at[0], gathered.at[pl.ds(chip * SHARD, SHARD)], own_sem)
-    own.start()
+    def source(r):
+        return chip_at([back[d][((r >> d) & 1) + 2 * ((r >> (3 + d)) & 1)] for d in range(3)])
+
+    neighbour = [source(1 << link) for link in range(6)]
+
+    own = [
+        pltpu.make_async_copy(
+            omega.at[0, pl.ds(pl.multiple_of(REST * odd + d * THIRD, UNIT), THIRD)],
+            thirds.at[pl.ds(d * (CHIPS // 2) * THIRD, THIRD)],
+            own_sem.at[d],
+        )
+        for d in range(3)
+    ]
+    own.append(
+        pltpu.make_async_copy(
+            omega.at[0, pl.ds(pl.multiple_of(3 * THIRD * (1 - odd), UNIT), REST)],
+            rests.at[pl.ds(pl.multiple_of(REST * odd, UNIT), REST)],
+            own_sem.at[3],
+        )
+    )
+    for copy in own:
+        copy.start()
     barrier = pltpu.get_barrier_semaphore()
-    for there in neighbour.values():
+    for there in neighbour:
         pl.semaphore_signal(barrier, inc=1, device_id=(child, there), device_id_type=MESH)
     pl.semaphore_signal(barrier, inc=1, device_id=(1 - child, chip), device_id_type=MESH)
 
-    def walk(i):
-        return i + i // 2 - 2 * (i // 3)
-
-    def pair_of(batch, i):
-        other, ny, nz, y0, z0 = batch
-        y = lax.rem(place[1] + SIDE - walk(y0 + lax.rem(i, ny)), SIDE)
-        z = lax.rem(place[2] + SIDE - walk(z0 + i // ny), SIDE)
-        half = place[0] // 2
-        half = 1 - half if other else half
-        return (z * SIDE + y) * 2 + half
-
-    def slab_copy(batch, first, i):
-        columns = pl.ds(pl.multiple_of(pair_of(batch, i) * PAIR, PAIR), PAIR)
-        return pltpu.make_async_copy(front.at[0, :, columns], slab.at[first + i], slab_sem.at[first + i])
-
-    firsts, count = [], 0
-    for batch in BATCHES:
-        firsts.append(count)
-        count += batch[1] * batch[2]
+    def coordinates(r):
+        found = []
+        for d in range(3):
+            v = place[d]
+            v = v + lax.rem(r // (1 << d), 2) * (1 - 2 * lax.rem(v, 2))
+            found.append(v + lax.rem(r // (1 << (3 + d)), 2) * (3 - 2 * v))
+        return found
+
+    def t_copy(r):
+        xyz = coordinates(r)
+        at = (chip_at(xyz) // 2) * PAIR + lax.rem(xyz[0], 2) * (3 * THIRD + 2 * REST)
+        return pltpu.make_async_copy(
+            front.at[0, :, pl.ds(pl.multiple_of(at, 128), 3 * THIRD)], slab_t.at[r], t_sem.at[r]
+        )
+
+    def r_copy(idx):
+        at = (chip_at(coordinates(2 * idx)) // 2) * PAIR + 3 * THIRD
+        return pltpu.make_async_copy(
+            front.at[0, :, pl.ds(pl.multiple_of(at, 128), 2 * REST)], slab_r.at[idx], r_sem.at[idx]
+        )
+
+    def each(first, count, step):
+        def one(i, carry):
+            step(i)
+            return carry
+
+        lax.fori_loop(first, first + count, one, 0)
+
     inputs = [
         pltpu.make_async_copy(source_ref, kept, in_sem.at[i])
         for i, (source_ref, kept) in enumerate(
@@ -169,37 +216,66 @@
         )
     ]
 
+    each(0, CHIPS, lambda r: t_copy(r).start())
+
     def start_loads():
         for copy in inputs:
             copy.start()
-        for batch, first in zip(BATCHES, firsts):
-
-            def start(i, carry, batch=batch, first=first):
-                slab_copy(batch, first, i).start()
-                return carry
-
-            lax.fori_loop(0, batch[1] * batch[2], start, 0)
+        each(0, CHIPS // 2, lambda idx: r_copy(idx).start())
         total[...] = jnp.zeros_like(total)
-
-    def piece(offset, part, half):
-        return gathered.at[pl.ds(source(offset) * SHARD + part * (2 * PIECE) + half * PIECE, PIECE)]
-
-    def wait_slot(t):
-        some = gathered.at[pl.ds(0, 6 * PIECE)]
+        partial[...] = jnp.zeros_like(partial)
+
+    def piece(name, r, base):
+        kind, d, h = name
+        if kind == "T":
+            return thirds.at[pl.ds((d * (CHIPS // 2) + drop_bit(r, d)) * THIRD + h * (THIRD // 2), THIRD // 2)]
+        parity = odd if (base & 1) == ((base >> 3) & 1) else 1 - odd
+        at = (r >> 1) * (2 * REST) + d * UNIT + REST * parity
+        return rests.at[pl.ds(pl.multiple_of(at, UNIT), UNIT)]
+
+    def send(t, link, name, r):
+        kind, d, _ = name
+        if kind == "F":
+            data = slab_t.at[r, :, pl.ds(d * THIRD, THIRD)]
+            into = lent.at[d * (CHIPS // 2) + drop_bit(r, d)]
+        elif kind == "S":
+            data, into = partial.at[d], came.at[d]
+        else:
+            data, into = piece(name, r, r), piece(name, r ^ (1 << link), r)
         pltpu.make_async_remote_copy(
-            some, some, sent_sem, slot_sem.at[t], device_id=(child, neighbour[0, 1]), device_id_type=MESH
-        ).wait_recv()
-
-    def multiply(number):
-        batch, first = BATCHES[number], firsts[number]
-
-        def one(i, carry):
-            slab_copy(batch, first, i).wait()
-            some = pl.ds(pl.multiple_of(pair_of(batch, i) * PAIR, PAIR), PAIR)
-            total[...] += jnp.dot(slab[first + i], gathered[some, :], preferred_element_type=jnp.float32)
-            return carry
-
-        lax.fori_loop(0, batch[1] * batch[2], one, 0)
+            data, into, sent_sem.at[link], slot_sem.at[t], device_id=(child, neighbour[link]), device_id_type=MESH
+        ).start()
+
+    def wait_units(units, sent, arrival):
+        some = thirds.at[pl.ds(0, units * UNIT)]
+        return pltpu.make_async_remote_copy(
+            some, some, sent, arrival, device_id=(child, neighbour[0]), device_id_type=MESH
+        )
+
+    def multiply_t(batch):
+        d, first, count = batch
+
+        def two(i):
+            low = 1 << d
+            r = [(idx // low) * (2 * low) + lax.rem(idx, low) for idx in (2 * i, 2 * i + 1)]
+            at = (d * (CHIPS // 2) + 2 * i) * THIRD
+            right = thirds[pl.ds(pl.multiple_of(at, THIRD), 2 * THIRD), :]
+            left = jnp.concatenate([slab_t[r[0], :, d * THIRD : (d + 1) * THIRD], slab_t[r[1], :, d * THIRD : (d + 1) * THIRD]], axis=1)
+            total[...] += jnp.dot(left, right, preferred_element_type=jnp.float32)
+            left = jnp.concatenate([lent[d * (CHIPS // 2) + 2 * i], lent[d * (CHIPS // 2) + 2 * i + 1]], axis=1)
+            partial[d] += jnp.dot(left, right, preferred_element_type=jnp.float32)
+
+        each(first // 2, count // 2, two)
+
+    def multiply_r(batch):
+        first, count = batch
+
+        def one(idx):
+            r_copy(idx).wait()
+            right = rests[pl.ds(pl.multiple_of(idx * (2 * REST), 2 * REST), 2 * REST), :]
+            total[...] += jnp.dot(slab_r[idx], right, preferred_element_type=jnp.float32)
+
+        each(first, count, one)
 
     def clear():
         recv1[...] = jnp.zeros_like(recv1)
@@ -347,27 +423,32 @@
     jobs += over_groups(p4_group)
     jobs += [own_rows]
 
-    own.wait()
+    for copy in own:
+        copy.wait()
     pl.semaphore_wait(barrier, 7)
-    slots, arrived = make_schedule(WINDOW)
-    ready = [ready_slot(batch, arrived) for batch in BATCHES]
-    done = 0
-    for t in range(len(slots) + WINDOW):
+    steps, arrived = make_schedule(WINDOW)
+    pending = [(t_ready(batch, arrived), multiply_t, batch) for batch in T_BATCHES]
+    pending += [(r_ready(batch, arrived), multiply_r, batch) for batch in R_BATCHES]
+    pending.sort(key=lambda entry: entry[0])
+    sent_units = [0] * 6
+    for t in range(len(steps) + WINDOW):
         if t >= WINDOW:
-            wait_slot(t - WINDOW)
-        if t < len(slots):
-            for link, offset, part, half in slots[t]:
-                data = piece(offset, part, half)
-                pltpu.make_async_remote_copy(
-                    data, data, sent_sem, slot_sem.at[t], device_id=(child, neighbour[link]), device_id_type=MESH
-                ).start()
-        if t >= WINDOW - 1 and jobs:
+            units = sum(size for _, _, _, size in steps[t - WINDOW])
+            wait_units(units, sent_sem.at[0], slot_sem.at[t - WINDOW]).wait_recv()
+        if loaded_step(0) <= t <= loaded_step(CHIPS - 1):
+            each(16 * (t - loaded_step(0)), 16, lambda r: t_copy(r).wait())
+        if t < len(steps):
+            for link, name, r, size in steps[t]:
+                send(t, link, name, r)
+                sent_units[link] += size
+        if t >= WINDOW - 2 and jobs:
             jobs.pop(0)()
-        if t == len(slots) + WINDOW - 1:
+        if t == len(steps) + WINDOW - 1:
             pl.semaphore_signal(mate_sem, inc=1, device_id=(1 - child, chip), device_id_type=MESH)
-        while done < len(BATCHES) and ready[done] <= t - WINDOW:
-            multiply(done)
-            done += 1
+        while pending and pending[0][0] <= t - WINDOW:
+            _, multiply, batch = pending.pop(0)
+            multiply(batch)
+    total[...] += came[0] + came[1] + came[2]
 
     def fill(send, picker, values):
         both = two_parts(values)
@@ -392,7 +473,7 @@
 
     def exchange(send, recv, sent_sem, came_sem):
         for _, dx, dy, dz, other in order:
-            to = source((dx, dy, dz))
+            to = chip_at([lax.rem(place[i] + v, SIDE) for i, v in enumerate((dx, dy, dz))])
             kid = 1 - child if other else child
             pltpu.make_async_remote_copy(
                 send.at[kid * CHIPS + to, used],
@@ -409,7 +490,7 @@
             recv.at[most, used],
             sent_sem,
             came_sem,
-            device_id=(child, neighbour[0, 1]),
+            device_id=(child, neighbour[0]),
             device_id_type=MESH,
         )
 
@@ -433,17 +514,15 @@
         out_rows[here(side), :] = picked(p4[...], parts[...])
     for copy in first + second:
         copy.wait_send()
-    sent = gathered.at[pl.ds(0, 6 * PIECE * len(slots))]
-    pltpu.make_async_remote_copy(
-        sent, sent, sent_sem, slot_sem.at[0], device_id=(child, neighbour[0, 1]), device_id_type=MESH
-    ).wait_send()
+    for link in range(6):
+        wait_units(sent_units[link], sent_sem.at[link], slot_sem.at[0]).wait_send()
 
 
 def body(front_update, child_omega, parent_block, parent_omega, child_map, leaf_order):
     local_rows = front_update.shape[1]
     sample_cols = child_omega.shape[2]
     parent_dev, leaf_size = parent_block.shape
-    slots, _ = make_schedule(WINDOW)
+    steps, _ = make_schedule(WINDOW)
     vmem = pl.BlockSpec(memory_space=pltpu.VMEM)
     anywhere = pl.BlockSpec(memory_space=pl.ANY)
     tiles = pltpu.VMEM((2, OWNERS, TILE, 128), jnp.float32)
@@ -455,9 +534,14 @@
         in_specs=[anywhere] * 6,
         out_specs=vmem,
         scratch_shapes=[
-            pltpu.VMEM((CHIPS * SHARD, sample_cols), jnp.bfloat16),
-            pltpu.VMEM((CHIPS // 2, local_rows, PAIR), jnp.bfloat16),
+            pltpu.VMEM((3 * (CHIPS // 2) * THIRD, sample_cols), jnp.bfloat16),
+            pltpu.VMEM((CHIPS * REST, sample_cols), jnp.bfloat16),
+            pltpu.VMEM((CHIPS, local_rows, 3 * THIRD), jnp.bfloat16),
+            pltpu.VMEM((CHIPS // 2, local_rows, 2 * REST), jnp.bfloat16),
+            pltpu.VMEM((3 * (CHIPS // 2), local_rows, THIRD), jnp.bfloat16),
             pltpu.VMEM((local_rows, sample_cols), jnp.float32),
+            pltpu.VMEM((3, local_rows, sample_cols), jnp.float32),
+            pltpu.VMEM((3, local_rows, sample_cols), jnp.float32),
             pltpu.VMEM((2 * parent_dev, 128), jnp.float32),
             pltpu.VMEM((slot_rows, 256), jnp.bfloat16),
             tiles,
@@ -475,11 +559,12 @@
             pltpu.VMEM((OWNERS // 2, 2 * local_rows), jnp.int32),
             pltpu.VMEM((2 * CAP, OWNERS, 128), jnp.float32),
             pltpu.VMEM((128, parent_dev), jnp.float32),
-            dma,
+            dma((4,)),
+            dma((CHIPS,)),
             dma((CHIPS // 2,)),
             dma((4,)),
-            dma,
-            dma((len(slots),)),
+            dma((6,)),
+            dma((len(steps),)),
             pltpu.SemaphoreType.REGULAR,
             dma((2,)),
             dma((2,)),

time: 142 us -> 137 us (0.965)
  Pallas kernels: 140 us -> 135 us
    pallas_call x1, Pallas kernels: 140 us -> 135 us  [body(): pl.pallas_call(kernel, out_shape=jax.ShapeDtypeStruct((2 * parent_dev, 12...]
where the time goes in v5:
time: 137 us
  Pallas kernels  135 us (99%)
    pallas_call x1, Pallas kernels, body(): pl.pallas_call(kernel, out_shape=jax.ShapeDtypeStruct((2 * parent_dev, 12...  135 us

profile of v5, /device:TPU:1, one launch (start us, length us, event | category | flops | bytes accessed | tf_op | source)
XLA Modules:
  0.0 137.3 jit_solution(17148281861260742288)
XLA Ops:
  0.0 135.4 %shard_map.64 = f32[768,128]{1,0:T(8,128)} custom-call(bf16[1,192,61440]{2,1,0:T(8,128)(2,1)} %front.1, bf16[1,960,256]{2,1,0:T(8,128)(2,1)} %omega.1, bf16[384,128]{1,0:T(8,128)(2,1)} %block_in.1, bf16[384,256]{1,0:T(8,128)(2,1)} %parent_in.1, s32[2,12288]{1,0:T(2,128)} %child_map.1, s32[384,128]{1,0:T(8,128)} %bitcast.1), custom_call_target="tpu_custom_call" | custom-call | tf_op jit(solution)/shard_map/pallas_call | solution.py:531
  135.4 1.0 fusion
  136.5 0.8 pad_maximum_fusion

commit v6 on v5

--- a/solution.py
+++ b/solution.py
@@ -17,7 +17,7 @@
 PAIR = 2 * SHARD
 CAP = 3
 TILE = 8
-WINDOW = 4
+WINDOW = 7
 UNIT = 64
 STEP = 2
 
@@ -34,7 +34,7 @@
             found.append((("T", d, h), links, (0.0, 1.0, 2.0, 3.0, 4.0), 2))
     for i in range(3):
         b, c = (i + 1) % 3, (i + 2) % 3
-        found.append((("R", i, 0), (i, b, 3 + i, 3 + b, c, 3 + c), (0.5, 1.5, 2.5, 3.5, 3.7, 9.0), 1))
+        found.append((("R", i, 0), (i, 3 + i, b, 3 + b, c, 3 + c), (0.5, 1.5, 2.5, 3.5, 3.7, 9.0), 1))
     return found
 
 
@@ -51,7 +51,6 @@
         for r in range(CHIPS):
             if (r >> d) & 1:
                 sends[d].append((5.0, (0, 0, drop_bit(r, d)), ("F", d, 0), r, 3))
-        sends[d].append((6.0, (0, 0, 0), ("S", d, 0), 0, 6))
     return [sorted(found) for found in sends]
 
 
@@ -59,7 +58,7 @@
     return 3 + r // 16
 
 
-T_BATCHES = tuple((d, 8 * g, 8) for g in range(4) for d in range(3))
+T_BATCHES = tuple((d, 8 * g, 8) for g in range(3) for d in range(3)) + tuple((d, first, count) for first, count in ((24, 4), (28, 2), (30, 2)) for d in range(3))
 R_BATCHES = tuple((4 * m, 4) for m in (0, 1, 2, 4, 3, 5, 6)) + tuple((28 + i, 1) for i in range(4))
 
 
@@ -98,9 +97,6 @@
                     _, _, name, r, size = item
                     if name[0] == "F":
                         fit = loaded_step(r) <= t
-                    elif name[0] == "S":
-                        last = max(t_ready(b, arrived) for b in T_BATCHES if b[0] == name[1])
-                        fit = last + window + 1 <= t
                     else:
                         fit = arrived.get((name, r), 10**6) + window <= t
                     if fit:
@@ -136,7 +132,7 @@
     front, omega, block_in, parent_in, child_map, leaf_order, out_rows,
     thirds, rests, slab_t, slab_r, lent, total, partial, came, stacked, parts, send1, recv1, send2, recv2, p1, p2, p3, p4,
     block, parent_omega, map_rows, leaf_rows, map_table, columns, scratch,
-    own_sem, t_sem, r_sem, in_sem, sent_sem, slot_sem, mate_sem, sent1, came1, sent2, came2,
+    own_sem, t_sem, r_sem, in_sem, sent_sem, back_sem, slot_sem, mate_sem, sent1, came1, sent2, came2,
 ):
     child = lax.axis_index("child")
     chip = lax.axis_index("rows")
@@ -238,13 +234,21 @@
         if kind == "F":
             data = slab_t.at[r, :, pl.ds(d * THIRD, THIRD)]
             into = lent.at[d * (CHIPS // 2) + drop_bit(r, d)]
-        elif kind == "S":
-            data, into = partial.at[d], came.at[d]
         else:
             data, into = piece(name, r, r), piece(name, r ^ (1 << link), r)
         pltpu.make_async_remote_copy(
             data, into, sent_sem.at[link], slot_sem.at[t], device_id=(child, neighbour[link]), device_id_type=MESH
         ).start()
+
+    def lend_back(d):
+        return pltpu.make_async_remote_copy(
+            partial.at[d],
+            came.at[d],
+            back_sem.at[0, d],
+            back_sem.at[1, d],
+            device_id=(child, neighbour[d]),
+            device_id_type=MESH,
+        )
 
     def wait_units(units, sent, arrival):
         some = thirds.at[pl.ds(0, units * UNIT)]
@@ -448,7 +452,11 @@
         while pending and pending[0][0] <= t - WINDOW:
             _, multiply, batch = pending.pop(0)
             multiply(batch)
-    total[...] += came[0] + came[1] + came[2]
+            if multiply is multiply_t and batch[1] + batch[2] == CHIPS // 2:
+                lend_back(batch[0]).start()
+    for d in range(3):
+        lend_back(d).wait_recv()
+        total[...] += came[d]
 
     def fill(send, picker, values):
         both = two_parts(values)
@@ -514,6 +522,8 @@
         out_rows[here(side), :] = picked(p4[...], parts[...])
     for copy in first + second:
         copy.wait_send()
+    for d in range(3):
+        lend_back(d).wait_send()
     for link in range(6):
         wait_units(sent_units[link], sent_sem.at[link], slot_sem.at[0]).wait_send()
 
@@ -564,6 +574,7 @@
             dma((CHIPS // 2,)),
             dma((4,)),
             dma((6,)),
+            dma((2, 3)),
             dma((len(steps),)),
             pltpu.SemaphoreType.REGULAR,
             dma((2,)),

time: 137 us -> 135 us (0.985)
  Pallas kernels: 135 us -> 133 us
    pallas_call x1, Pallas kernels: 135 us -> 133 us  [body(): pl.pallas_call(kernel, out_shape=jax.ShapeDtypeStruct((2 * parent_dev, 12...]
where the time goes in v6:
time: 135 us
  Pallas kernels  133 us (99%)
    pallas_call x1, Pallas kernels, body(): pl.pallas_call(kernel, out_shape=jax.ShapeDtypeStruct((2 * parent_dev, 12...  133 us

profile of v6, /device:TPU:1, one launch (start us, length us, event | category | flops | bytes accessed | tf_op | source)
XLA Modules:
  0.0 134.8 jit_solution(15691453963994960161)
XLA Ops:
  0.0 133.0 %shard_map.64 = f32[768,128]{1,0:T(8,128)} custom-call(bf16[1,192,61440]{2,1,0:T(8,128)(2,1)} %front.1, bf16[1,960,256]{2,1,0:T(8,128)(2,1)} %omega.1, bf16[384,128]{1,0:T(8,128)(2,1)} %block_in.1, bf16[384,256]{1,0:T(8,128)(2,1)} %parent_in.1, s32[2,12288]{1,0:T(2,128)} %child_map.1, s32[384,128]{1,0:T(8,128)} %bitcast.1), custom_call_target="tpu_custom_call" | custom-call | tf_op jit(solution)/shard_map/pallas_call | solution.py:541
  133.0 1.0 fusion
  134.0 0.8 pad_maximum_fusion

commit v7 on v6

--- a/solution.py
+++ b/solution.py
@@ -34,7 +34,7 @@
             found.append((("T", d, h), links, (0.0, 1.0, 2.0, 3.0, 4.0), 2))
     for i in range(3):
         b, c = (i + 1) % 3, (i + 2) % 3
-        found.append((("R", i, 0), (i, 3 + i, b, 3 + b, c, 3 + c), (0.5, 1.5, 2.5, 3.5, 3.7, 9.0), 1))
+        found.append((("R", i, 0), (3 + i, i, b, 3 + b, c, 3 + c), (0.5, 1.5, 2.5, 3.5, 3.7, 9.0), 1))
     return found
 
 

time: 135 us -> 134 us (level)
  no operation moved by 1% of the time
where the time goes in v7:
time: 134 us
  Pallas kernels  132 us (99%)
    pallas_call x1, Pallas kernels, body(): pl.pallas_call(kernel, out_shape=jax.ShapeDtypeStruct((2 * parent_dev, 12...  132 us

profile of v7, /device:TPU:1, one launch (start us, length us, event | category | flops | bytes accessed | tf_op | source)
XLA Modules:
  0.0 134.1 jit_solution(2220552360552446331)
XLA Ops:
  0.0 132.3 %shard_map.64 = f32[768,128]{1,0:T(8,128)} custom-call(bf16[1,192,61440]{2,1,0:T(8,128)(2,1)} %front.1, bf16[1,960,256]{2,1,0:T(8,128)(2,1)} %omega.1, bf16[384,128]{1,0:T(8,128)(2,1)} %block_in.1, bf16[384,256]{1,0:T(8,128)(2,1)} %parent_in.1, s32[2,12288]{1,0:T(2,128)} %child_map.1, s32[384,128]{1,0:T(8,128)} %bitcast.1), custom_call_target="tpu_custom_call" | custom-call | tf_op jit(solution)/shard_map/pallas_call | solution.py:541
  132.3 1.0 fusion
  133.3 0.8 pad_maximum_fusion
